TPU v7x, 128 devices: a whole 4x4x4 slice. The times are simulated.
128 devices in a mesh: tp: 4 (over y_hi, core), grp: 32 (over z, x, y_lo).
Axes of the slice: x: 4, y: 4 (y_hi: 2, y_lo: 2; y = y_hi * 2 + y_lo), z: 4, core: 2. Of those that a mesh axis runs over, the one named last changes fastest.
Arguments:
- teacher_state: bfloat16 [8192, 5280], P('grp'), may hold values from -6 to 6
- injection: bfloat16 [8192, 5280], P('grp'), may hold values from -6 to 6
- teacher_up: bfloat16 [5280, 8960], P(None, 'tp'), may hold values from -0.078125 to 0.078125
- teacher_down: bfloat16 [8960, 5280], P('tp', 'grp'), may hold values from -0.0625 to 0.0625
- student_up: bfloat16 [5280, 256], P('grp', 'tp'), may hold values from -0.078125 to 0.078125
- student_down: bfloat16 [256, 5280], P('tp', 'grp'), may hold values from -0.375 to 0.375
- teacher_step: int32 [8], replicated, may hold values from 0 to 1
- student_depth: int32 [8], replicated, may hold values from 1 to 2
Outputs:
- grad_up: float32 [5280, 256], P('grp', 'tp')
- grad_down: float32 [256, 5280], P('tp', 'grp')
All inputs are finite; a program needn't handle non-finite values.
Results may differ from a plain program's by a relative error of at most 0.02.
Values may be sent and summed in bfloat16 or wider, within the bound.
A program may use at most 192 MiB of HBM per device.

v0:
```python
import jax
import jax.numpy as jnp
from jax import lax
from jax.sharding import PartitionSpec as P

LENGTH = 1024
S_ITERS = 2


epsilon = 1e-06
loss_scale = 64.0


def in_order(tiles, dim):
    shape = list(tiles.shape[1:])
    shape[dim] *= tiles.shape[0]
    return jnp.moveaxis(tiles, 0, dim).reshape(shape)


def on_gathered_pieces(value, axis, dim, apply, out_dim):
    size, extent = (lax.axis_size(axis), value.shape[dim])
    count = 2 if extent % 2 == 0 else 1
    outs, length = ([], extent // count)
    for k in range(count):
        piece = lax.slice_in_dim(value, k * length, (k + 1) * length, axis=dim)
        starts = jnp.arange(size) * extent + k * length
        outs.append(jax.vmap(apply)(lax.all_gather(piece, axis), starts))
    return in_order(jnp.concatenate(outs, axis=out_dim + 1), out_dim)


def in_blocks(value, dim, size):
    shape = value.shape
    tiles = value.reshape(*shape[:dim], size, shape[dim] // size, *shape[dim + 1 :])
    return jnp.moveaxis(tiles, dim, 0)


def sent_and_summed(value, axis, dim):
    tiles = in_blocks(value, dim, lax.axis_size(axis))
    arrived = lax.all_to_all(tiles, axis, split_axis=0, concat_axis=0, tiled=True)
    return arrived.astype(jnp.float32).sum(axis=0)


def normalize(summed):
    return lax.rsqrt(jnp.mean(summed * summed, axis=-1, keepdims=True) + epsilon)


def silu_slope(logits):
    sigmoid = jax.nn.sigmoid(logits)
    return sigmoid * (1.0 + logits * (1.0 - sigmoid))


def student_grads(
    start, injection, latents, pick_teacher, pick_depth, student_up, student_down, row_count
):
    previous = start
    records = []
    outputs = []
    for iteration in range(S_ITERS):
        summed = previous.astype(jnp.float32) + injection.astype(jnp.float32)
        factor = normalize(summed)
        normed = (summed * factor).astype(jnp.bfloat16)
        logits = jnp.dot(normed, student_up, preferred_element_type=jnp.float32)
        hidden = jax.nn.silu(logits).astype(jnp.bfloat16)
        previous = (
            previous.astype(jnp.float32)
            + jnp.dot(hidden, student_down, preferred_element_type=jnp.float32)
        ).astype(jnp.bfloat16)
        records.append((summed, factor, normed, logits, hidden))
        outputs.append(previous)
    target = start.astype(jnp.float32)
    iteration = 0
    target = jnp.where(
        pick_teacher[:, None] == iteration + 1, latents[iteration].astype(jnp.float32), target
    )
    result = jnp.zeros(start.shape, jnp.float32)
    for iteration in range(S_ITERS):
        result = jnp.where(
            pick_depth[:, None] == iteration + 1, outputs[iteration].astype(jnp.float32), result
        )
    slope = loss_scale * 2.0 / row_count * (result - target)
    grad_up = jnp.zeros(student_up.shape, jnp.float32)
    grad_down = jnp.zeros(student_down.shape, jnp.float32)
    carried = jnp.zeros(start.shape, jnp.float32)
    for iteration in reversed(range(S_ITERS)):
        summed, factor, normed, logits, hidden = records[iteration]
        cotangent = carried + jnp.where(pick_depth[:, None] == iteration + 1, slope, 0.0)
        rounded = cotangent.astype(jnp.bfloat16)
        grad_down = grad_down + jnp.dot(hidden.T, rounded, preferred_element_type=jnp.float32)
        upstream = jnp.dot(rounded, student_down.T, preferred_element_type=jnp.float32)
        local_grad = (upstream * silu_slope(logits)).astype(jnp.bfloat16)
        grad_up = grad_up + jnp.dot(normed.T, local_grad, preferred_element_type=jnp.float32)
        if iteration > 0:
            back_flow = jnp.dot(local_grad, student_up.T, preferred_element_type=jnp.float32)
            carried = (
                cotangent
                + factor * back_flow
                - summed * factor**3 * jnp.mean(summed * back_flow, axis=-1, keepdims=True)
            )
    return (grad_up, grad_down)


def body(
    teacher_state,
    injection,
    teacher_up,
    teacher_down,
    student_up,
    student_down,
    teacher_step,
    student_depth,
):
    slices = lax.axis_size("tp")
    group_rows = teacher_state.shape[0]
    own_count = group_rows // slices
    row_start = lax.axis_index("tp") * own_count

    def own_rows(whole):
        return lax.dynamic_slice_in_dim(whole, row_start, own_count, 0)

    latents = []
    summed = teacher_state.astype(jnp.float32) + injection.astype(jnp.float32)
    normed = (summed * normalize(summed)).astype(jnp.bfloat16)
    hidden = jax.nn.silu(jnp.dot(normed, teacher_up, preferred_element_type=jnp.float32)).astype(
        jnp.bfloat16
    )

    def columns(piece, start):
        return jnp.dot(hidden, piece, preferred_element_type=jnp.float32)

    row_share = lax.psum_scatter(
        on_gathered_pieces(teacher_down, "grp", 1, columns, 1).astype(jnp.bfloat16),
        "tp",
        scatter_dimension=0,
        tiled=True,
    ).astype(jnp.float32)
    row_state = (own_rows(teacher_state).astype(jnp.float32) + row_share).astype(jnp.bfloat16)
    latents.append(row_state)
    gathered_up, gathered_down = (
        lax.all_gather(student_up, "grp", axis=0, tiled=True),
        lax.all_gather(student_down, "grp", axis=1, tiled=True),
    )
    gathered_up, gathered_down = (
        lax.all_gather(gathered_up, "tp", axis=1, tiled=True),
        lax.all_gather(gathered_down, "tp", axis=0, tiled=True),
    )
    first_row = lax.axis_index("grp") * group_rows + row_start
    sequence = (first_row + jnp.arange(own_count, dtype=jnp.int32)) // LENGTH
    matches = sequence[:, None] == jnp.arange(teacher_step.shape[0], dtype=jnp.int32)[None, :]
    pick_teacher = jnp.sum(jnp.where(matches, teacher_step[None, :], 0), axis=1)
    pick_depth = jnp.sum(jnp.where(matches, student_depth[None, :], 0), axis=1)
    grad_up, grad_down = student_grads(
        own_rows(teacher_state),
        own_rows(injection),
        latents,
        pick_teacher,
        pick_depth,
        gathered_up,
        gathered_down,
        group_rows * lax.axis_size("grp"),
    )
    grad_up, grad_down = (
        lax.psum_scatter(
            grad_up.astype(jnp.bfloat16), "tp", scatter_dimension=1, tiled=True
        ).astype(jnp.float32),
        lax.psum_scatter(
            grad_down.astype(jnp.bfloat16), "tp", scatter_dimension=0, tiled=True
        ).astype(jnp.float32),
    )
    grad_up, grad_down = (
        sent_and_summed(grad_up.astype(jnp.bfloat16), "grp", 0),
        sent_and_summed(grad_down.astype(jnp.bfloat16), "grp", 1),
    )
    return (grad_up, grad_down)


def solution(mesh):
    in_specs = (
        P("grp", None),
        P("grp", None),
        P(None, "tp"),
        P("tp", "grp"),
        P("grp", "tp"),
        P("tp", "grp"),
        P(),
        P(),
    )
    out_specs = (P("grp", "tp"), P("tp", "grp"))
    return jax.shard_map(body, mesh=mesh, in_specs=in_specs, out_specs=out_specs, check_vma=False)
```

profile of v0, /device:TPU:1, one launch (start us, length us, event | category | flops | bytes accessed | tf_op | source)
XLA Modules:
  0.0 828.0 jit_solution(9276407297608392390)
XLA Ops:
  7.2 0.0 all-gather.12.cloned.1.call-start
  7.2 0.7 all-gather.12.cloned.1.call-update
  7.9 0.0 all-gather.8.cloned.1.call-start
  7.9 101.3 %all-gather.1 = bf16[32,165,64]{1,2,0:T(8,128)(2,1)S(1)} all-gather(bf16[1,165,64]{1,2,0:T(8,128)(2,1)} %bitcast.37), channel_id=1, replica_groups=mesh['tp'=4,'grp'=32] {'grp'}, dimensions={0}, use_global_device_ids=true | all-gather | bytes 696960 | tf_op jit(solution)/shard_map/all_gather | solution.py:139
  109.2 0.6 copy.27
  109.8 2.3 reshape.83
  112.1 0.0 all-gather.8.cloned.1.call-update
  112.1 0.0 all-gather.10.cloned.1.call-start
  112.2 99.8 %all-gather.2 = bf16[32,165,64]{1,2,0:T(8,128)(2,1)S(1)} all-gather(bf16[1,165,64]{1,2,0:T(8,128)(2,1)S(1)} %bitcast.38), channel_id=1, replica_groups=mesh['tp'=4,'grp'=32] {'grp'}, dimensions={0}, use_global_device_ids=true | all-gather | bytes 696960 | tf_op jit(solution)/shard_map/all_gather | solution.py:140
  212.0 1.6 copy.28
  213.5 3.1 reshape.85
  216.6 0.0 all-gather.10.cloned.1.call-update
  216.6 0.2 reduce-scatter.4.cloned.1.call-start
  216.9 0.0 copy-start.10
  216.9 2.9 multiply_reduce_fusion
  219.8 13.2 %fusion.11 = bf16[256,2240,1]{0,1,2:T(8,128)(2,1)} fusion(bf16[5280,2240]{0,1:T(8,128)(2,1)} %param.10, bf16[256,5280]{0,1:T(8,128)(2,1)S(1)} %copy-done.8, bf16[256,5280]{0,1:T(8,128)(2,1)S(1)} %copy-done.10, f32[256]{0:T(256)S(1)} %add_rsqrt_fusion), kind=kOutput, calls=%fused_computation.22 | convolution fusion | flops 6065152000 | bytes 30209024 | tf_op jit(solution)/shard_map/dot_general | solution.py:123
  233.1 351.1 %all-gather.12.cloned.1.call-done = bf16[32,2240,165]{1,2,0:T(8,128)(2,1)} async-done(((bf16[1,2240,165]{1,2,0:T(8,128)(2,1)}), bf16[32,2240,165]{1,2,0:T(8,128)(2,1)}) %all-gather.12.cloned.1.call-update) | async-done | bytes 23654416 | tf_op jit(solution)/shard_map/all_gather | solution.py:27
  584.2 12.8 %convolution_convert_fusion = bf16[256,32,165]{0,2,1:T(8,128)(2,1)} fusion(bf16[256,2240,1]{0,1,2:T(8,128)(2,1)} %fusion.11, bf16[32,2240,165]{1,2,0:T(8,128)(2,1)} %all-gather.12.cloned.1.call-done), kind=kOutput, calls=%fused_computation.23 | convolution fusion | flops 6056878080 | bytes 27504640 | tf_op jit(solution)/shard_map/vmap()/dot_general | solution.py:128
  597.0 3.0 convert_element_type.106
  600.1 3.2 copy.29
  603.3 0.0 reduce-scatter.4.cloned.1.call-update
  603.3 0.3 reduce-scatter.8.cloned.1.call-start
  603.6 1.5 copy-done.9
  605.1 3.7 constant_dynamic-slice_fusion
  608.8 1.8 copy.33
  610.6 1.0 copy.32
  611.7 0.1 select_reduce_fusion.1
  611.7 0.3 multiply_reduce_fusion.3
  612.1 7.5 all-gather.8.cloned.1.call-done
  619.6 2.7 fusion.22
  622.3 28.7 %all-gather.10.cloned.1.call-done = bf16[256,5280]{1,0:T(8,128)(2,1)} async-done(((bf16[64,5280]{1,0:T(8,128)(2,1)}), bf16[256,5280]{1,0:T(8,128)(2,1)}) %all-gather.10.cloned.1.call-update) | async-done | bytes 2703376 | tf_op jit(solution)/shard_map/all_gather | solution.py:144
  651.0 2.5 multiply_reduce_fusion.2
  653.5 0.5 multiply_multiply_fusion
  654.0 0.6 copy-done.1
  654.6 0.2 multiply_convert_fusion.7
  654.8 0.9 copy-done.6
  655.7 0.1 copy-done.3
  655.8 1.6 fusion.23
  657.4 37.3 %reduce-scatter.4.cloned.1.call-done = bf16[64,5280]{1,0:T(8,128)(2,1)} async-done(((bf16[256,5280]{1,0:T(8,128)(2,1)}), bf16[64,5280]{1,0:T(8,128)(2,1)}) %reduce-scatter.4.cloned.1.call-update) | async-done | bytes 675856 | tf_op jit(solution)/shard_map/reduce_scatter | solution.py:130
  694.7 2.5 fusion.8
  697.2 0.9 fusion.21
  698.1 1.0 fusion.13
  699.1 0.3 copy-done.2
  699.4 0.9 copy-done.4
  700.3 0.8 multiply_reduce_fusion.1
  701.1 0.6 add_convert_fusion
  701.7 0.9 copy-done.7
  702.5 2.5 fusion.1
  705.0 0.0 reduce-scatter.8.cloned.1.call-update
  705.0 0.3 reduce-scatter.6.cloned.1.call-start
  705.3 4.4 fusion.24
  709.8 7.7 fusion
  717.5 0.0 reduce-scatter.6.cloned.1.call-update
  717.5 29.3 %reduce-scatter.8.cloned.1.call-done = bf16[64,5280]{1,0:T(8,128)(2,1)} async-done(((bf16[256,5280]{1,0:T(8,128)(2,1)}), bf16[64,5280]{1,0:T(8,128)(2,1)}) %reduce-scatter.8.cloned.1.call-update) | async-done | bytes 675856 | tf_op jit(solution)/shard_map/reduce_scatter | solution.py:165
  746.8 4.1 reshape.80
  750.9 1.6 copy.35
  752.5 7.0 all-to-all-start.1
  759.5 32.4 %reduce-scatter.6.cloned.1.call-done = bf16[5280,64]{0,1:T(8,128)(2,1)} async-done(((bf16[5280,256]{0,1:T(8,128)(2,1)}), bf16[5280,64]{0,1:T(8,128)(2,1)}) %reduce-scatter.6.cloned.1.call-update) | async-done | bytes 675856 | tf_op jit(solution)/shard_map/reduce_scatter | solution.py:162
  791.9 4.1 reshape.79
  796.0 1.6 copy.30
  797.6 6.1 all-to-all-start
  803.7 0.8 convert_reduce_fusion
  804.6 15.8 %all-to-all-done = bf16[32,165,64]{1,2,0:T(8,128)(2,1)S(1)} async-done(((bf16[32,165,64]{1,2,0:T(8,128)(2,1)}), bf16[32,165,64]{1,2,0:T(8,128)(2,1)S(1)}, u32[]{:S(2)}, u32[]{:S(2)}) %all-to-all-start) | async-done | bytes 675872 | tf_op jit(solution)/shard_map/all_to_all | solution.py:39
  820.3 0.8 convert_reduce_fusion.1
  (32 shorter events, 0.1 us)
Async XLA Ops:
  7.2 577.0 %all-gather.12.cloned.1.call-start = ((), (), s32[]{:S(2)}) async-start(), calls=%async_computation.10 | async-start | bytes 25546752 | tf_op jit(solution)/shard_map/all_gather | solution.py:27
  7.9 611.7 %all-gather.8.cloned.1.call-start = ((), (), s32[]{:S(2)}) async-start(), calls=%async_computation.5 | async-start | bytes 3440640 | tf_op jit(solution)/shard_map/all_gather | solution.py:143
  109.2 2.9 copy-start.13
  112.1 538.9 %all-gather.10.cloned.1.call-start = ((), (), s32[]{:S(2)}) async-start(), calls=%async_computation.6 | async-start | bytes 3440640 | tf_op jit(solution)/shard_map/all_gather | solution.py:144
  212.0 4.9 copy-start.8
  216.6 478.0 %reduce-scatter.4.cloned.1.call-start = ((), (), s32[]{:S(2)}) async-start(), calls=%async_computation.7 | async-start | bytes 3440640 | tf_op jit(solution)/shard_map/reduce_scatter | solution.py:130
  216.9 2.9 copy-start.10
  603.3 1.8 copy-start.9
  603.3 143.5 %reduce-scatter.8.cloned.1.call-start = ((), (), s32[]{:S(2)}) async-start(), calls=%async_computation.9 | async-start | bytes 3440640 | tf_op jit(solution)/shard_map/reduce_scatter | solution.py:165
  608.8 1.8 copy-start.11
  608.8 2.9 copy-start.14
  608.8 2.9 copy-start.15
  611.6 39.4 %copy-start.5 = (bf16[64,5280]{1,0:T(8,128)(2,1)}, bf16[64,5280]{1,0:T(8,128)(2,1)S(1)}, u32[]{:S(2)}) copy-start(bf16[64,5280]{1,0:T(8,128)(2,1)S(1)} %copy.32) | copy-start | bytes 2027524
  653.5 1.1 copy-start.1
  653.5 2.3 copy-start.3
  654.8 0.9 copy-start.6
  655.8 38.9 %copy-start = (bf16[256,5280]{1,0:T(8,128)(2,1)S(1)}, bf16[256,5280]{1,0:T(8,128)(2,1)}, u32[]{:S(2)}) copy-start(bf16[256,5280]{1,0:T(8,128)(2,1)} %all-gather.10.cloned.1.call-done) | copy-start | bytes 8110084
  694.7 2.5 copy-start.12
  698.1 1.3 copy-start.2
  698.1 2.2 copy-start.4
  700.3 0.8 copy-start.16
  701.7 0.9 copy-start.7
  705.0 86.9 %reduce-scatter.6.cloned.1.call-start = ((), (), s32[]{:S(2)}) async-start(), calls=%async_computation.8 | async-start | bytes 3440640 | tf_op jit(solution)/shard_map/reduce_scatter | solution.py:162
  752.5 45.1 %all-to-all-start.1 = ((bf16[32,64,165]{2,1,0:T(8,128)(2,1)}), bf16[32,64,165]{2,1,0:T(8,128)(2,1)S(1)}, u32[]{:S(2)}, u32[]{:S(2)}) async-start(bf16[32,64,165]{2,1,0:T(8,128)(2,1)} %bitcast.34), calls=%async_computation.4 | async-start | bytes 2097152 | tf_op jit(solution)/shard_map/all_to_all | solution.py:39
  797.6 22.7 %all-to-all-start = ((bf16[32,165,64]{1,2,0:T(8,128)(2,1)}), bf16[32,165,64]{1,2,0:T(8,128)(2,1)S(1)}, u32[]{:S(2)}, u32[]{:S(2)}) async-start(bf16[32,165,64]{1,2,0:T(8,128)(2,1)} %copy.30), calls=%async_computation.2 | async-start | bytes 2097152 | tf_op jit(solution)/shard_map/all_to_all | solution.py:39
Sparse Core Ops, SparseCore 0:
  9.6 574.5 all-gather.11
  585.8 33.6 all-gather.7
  621.3 29.7 all-gather.9
  653.5 41.0 reduce-scatter.3
  705.1 41.6 reduce-scatter.7
  749.4 42.4 reduce-scatter.5
where the time goes:
time: 830 us; the launch traced here: 828 us
  waiting for transfers between devices  503 us (61%)
  blocking collectives  201 us (24%)
  matrix products  52.7 us (6%)
  local copies, waits for them, and re-layouts  36.7 us (4%)
  between operations  14.4 us (2%)
  starting transfers between devices  14 us (2%)
    all_gather x1, waiting for transfers between devices, on_gathered_pieces(): outs.append(jax.vmap(apply)(lax.all_gather(piece, axis), starts))  351 us
    all_gather x1, blocking collectives, body(): lax.all_gather(student_up, 'grp', axis=0, tiled=True)  101 us
    all_gather x1, blocking collectives, body(): lax.all_gather(student_down, 'grp', axis=1, tiled=True)  99.8 us
    reduce_scatter x1, waiting for transfers between devices, body(): lax.psum_scatter(on_gathered_pieces(teacher_down, 'grp', 1, columns, 1).a...  37.3 us
    reduce_scatter x1, waiting for transfers between devices, body(): lax.psum_scatter(grad_up.astype(jnp.bfloat16), 'tp', scatter_dimension=1,...  32.4 us
    reduce_scatter x1, waiting for transfers between devices, body(): lax.psum_scatter(grad_down.astype(jnp.bfloat16), 'tp', scatter_dimension=...  29.3 us
    all_gather x1, waiting for transfers between devices, body(): lax.all_gather(gathered_down, 'tp', axis=0, tiled=True)  28.7 us
  transfers between devices with their start and end apart: 8, of which 7 were waited for; matrix products, arithmetic and copies ran while one was open for 10% of the time, Pallas kernels for 0%

commit v1 on v0

v1 whole, which is shorter than its diff:
```python
import jax
import jax.numpy as jnp
from jax import lax
from jax.sharding import PartitionSpec as P

LENGTH = 1024
epsilon = 1e-06
loss_scale = 64.0
F32 = jnp.float32
BF16 = jnp.bfloat16


def dot(a, b, dims=((1,), (0,))):
    return lax.dot_general(a, b, (dims, ((), ())), preferred_element_type=F32)


def spread(block, axis):
    size = lax.axis_size(axis)
    tiles = jnp.broadcast_to(block[None], (size, *block.shape))
    return lax.all_to_all(tiles, axis, split_axis=0, concat_axis=0, tiled=True)


def exchange(tiles, axis):
    return lax.all_to_all(tiles, axis, split_axis=0, concat_axis=0, tiled=True)


def total_over(value, axis):
    size = lax.axis_size(axis)
    tiles = value.astype(BF16).reshape(size, value.shape[0] // size, value.shape[1])
    mine = exchange(tiles, axis).astype(F32).sum(axis=0).astype(BF16)
    return spread(mine, axis).reshape(value.shape)


def silu_slope(logits):
    sigmoid = jax.nn.sigmoid(logits)
    return sigmoid * (1.0 + logits * (1.0 - sigmoid))


def body(
    teacher_state,
    injection,
    teacher_up,
    teacher_down,
    student_up,
    student_down,
    teacher_step,
    student_depth,
):
    n_tp, n_grp = lax.axis_size("tp"), lax.axis_size("grp")
    tokens, width = teacher_state.shape
    cols, own = student_up.shape
    units = own * n_tp
    hidden = teacher_down.shape[0]
    scale = loss_scale * 2.0 / (tokens * n_grp)

    pair = jnp.concatenate([student_up.T, student_down], axis=0)
    pairs = spread(pair, "tp")
    up_cols = pairs[:, :own].reshape(units, cols)
    down_cols = pairs[:, own:].reshape(units, cols)
    pair_all = spread(pair, "grp")
    pair_all = jnp.moveaxis(pair_all, 0, 1).reshape(2 * own, width)

    right = jnp.concatenate([teacher_down.T, down_cols.T, up_cols.T], axis=1)
    small = total_over(dot(down_cols, right), "grp")
    teach = small[:, :hidden]
    gram = small[:, hidden : hidden + units]
    cross = small[:, hidden + units :]

    summed = teacher_state.T.astype(F32) + injection.T.astype(F32)
    square = jnp.sum(summed * summed, axis=0, keepdims=True)
    mean1 = square / width + epsilon
    rho1 = lax.rsqrt(mean1)
    norm1 = jnp.sqrt(mean1)
    normed = (summed * rho1).astype(BF16)

    mine = dot(pair_all, normed)
    both = spread(mine, "tp")
    logits1 = both[:, :own].reshape(units, tokens)
    along = both[:, own:].reshape(units, tokens) * norm1
    upward = logits1 * norm1

    teacher_hidden = jax.nn.silu(dot(teacher_up.T, normed)).astype(BF16)
    term = exchange(jnp.broadcast_to(dot(teach, teacher_hidden)[None], (n_tp, units, tokens)), "tp").sum(axis=0)

    first = lax.axis_index("grp") * tokens
    sequence = (first + jnp.arange(tokens, dtype=jnp.int32)) // LENGTH
    matches = sequence[None, :] == jnp.arange(teacher_step.shape[0], dtype=jnp.int32)[:, None]
    taught = jnp.sum(jnp.where(matches, teacher_step[:, None], 0), axis=0, keepdims=True) == 1
    deep = jnp.sum(jnp.where(matches, student_depth[:, None], 0), axis=0, keepdims=True) == 2

    hidden1 = jax.nn.silu(logits1).astype(BF16)
    gram1 = dot(gram, hidden1)
    hidden1_f = hidden1.astype(F32)
    moved = along + gram1
    square2 = square + jnp.sum(hidden1_f * (along + moved), axis=0, keepdims=True)
    rho2 = lax.rsqrt(jnp.maximum(square2, 0.0) / width + epsilon)
    upward2 = upward + dot(cross, hidden1, ((0,), (0,)))
    logits2 = upward2 * rho2
    hidden2 = jnp.where(deep, jax.nn.silu(logits2), 0.0).astype(BF16)
    total = (hidden1_f + hidden2.astype(F32)).astype(BF16)
    taught_total = jnp.where(taught, total, jnp.zeros_like(total))

    slope = scale * (gram1 + dot(gram, hidden2) - jnp.where(taught, term, 0.0))
    q2 = jnp.where(deep, slope * silu_slope(logits2), 0.0)
    mu = jnp.sum(upward2 * q2, axis=0, keepdims=True) / width
    rq2 = (rho2 * q2).astype(BF16)
    ratio = rho2 * rho2 * rho2 * mu
    slope1 = slope + dot(cross, rq2) - ratio * moved
    q1 = slope1 * silu_slope(logits1)

    start = lax.axis_index("tp") * own

    def mine_of(value):
        return lax.dynamic_slice_in_dim(value, start, own, 0)

    rq2_f = rq2.astype(F32)
    left = jnp.concatenate(
        [mine_of(q1 + rq2_f * norm1), mine_of(-hidden1_f * (ratio * norm1))], axis=0
    ).astype(BF16)
    partial = dot(left, normed, ((1,), (1,))).astype(BF16)
    partial = jnp.moveaxis(partial.reshape(2 * own, n_grp, cols), 1, 0)
    direct = exchange(partial, "grp").astype(F32).sum(axis=0)

    weighted = (hidden1_f * ratio).astype(BF16)
    nt = ((1,), (1,))
    c1 = scale * dot(mine_of(total), total, nt) - dot(mine_of(weighted), hidden1, nt)
    c2 = dot(mine_of(hidden1), rq2, nt)
    c3 = dot(mine_of(rq2), hidden1, nt)
    outer = -scale * dot(taught_total, teacher_hidden, nt)
    folded = jnp.concatenate([c1, c2, c3], axis=0).reshape(units, 3 * own)
    summed_all = total_over(jnp.concatenate([outer, folded], axis=1), "grp")
    folded = summed_all[:, hidden:].reshape(3 * own, units)
    through = dot(summed_all[:, :hidden], teacher_down)
    through = exchange(through.reshape(n_tp, own, cols), "tp").sum(axis=0)
    grad_down = direct[own:] + dot(folded[:own], down_cols) + dot(folded[own : 2 * own], up_cols) + through
    grad_up = direct[:own] + dot(folded[2 * own :], down_cols)
    return (grad_up.T, grad_down)


def solution(mesh):
    in_specs = (
        P("grp", None),
        P("grp", None),
        P(None, "tp"),
        P("tp", "grp"),
        P("grp", "tp"),
        P("tp", "grp"),
        P(),
        P(),
    )
    out_specs = (P("grp", "tp"), P("tp", "grp"))
    return jax.shard_map(body, mesh=mesh, in_specs=in_specs, out_specs=out_specs, check_vma=False)
```

time: 830 us -> 241 us (0.29)
  waiting for transfers between devices: 503 us -> 112 us
  blocking collectives: 201 us -> 0 us
  starting transfers between devices: 14 us -> 57.6 us
  local copies, waits for them, and re-layouts: 36.7 us -> 17.8 us
  matrix products: 52.7 us -> 34.4 us
  between operations: 14.4 us -> 0.9 us
  other arithmetic: 6.28 us -> 16.6 us
    all_gather x3 -> x0, waiting for transfers between devices: 387 us -> none  [the longest x1 351 us: on_gathered_pieces(): outs.append(jax.vmap(apply)(lax.all_gather(piece, axis), starts))]
    all_gather x2 -> x0, blocking collectives: 201 us -> none  [the longest x1 101 us: body(): lax.all_gather(student_up, 'grp', axis=0, tiled=True)]
    reduce_scatter x3 -> x0, waiting for transfers between devices: 99 us -> none  [the longest x1 37.3 us: body(): lax.psum_scatter(on_gathered_pieces(teacher_down, 'grp', 1, columns, 1).a...]
    all_to_all x2 -> x10, waiting for transfers between devices: 15.8 us -> 112 us  [the longest x5 59.7 us: exchange(): return lax.all_to_all(tiles, axis, split_axis=0, concat_axis=0, tiled=True)]
    all_to_all x2 -> x10, starting transfers between devices: 13.1 us -> 57.6 us  [the longest x5 30.6 us: spread(): return lax.all_to_all(tiles, axis, split_axis=0, concat_axis=0, tiled=True)]
    dot_general x12 -> x18, matrix products: 52.7 us -> 34.4 us  [dot(): return lax.dot_general(a, b, (dims, ((), ())), preferred_element_type=F32)]
    unnamed x38 -> x20, local copies, waits for them, and re-layouts: 13.2 us -> 0.69 us
  transfers between devices with their start and end apart: 8 -> 10, of which waited for: 7 -> 10; matrix products, arithmetic and copies ran while one was open for 10% -> 18% of each run, Pallas kernels for 0% -> 0%
where the time goes in v1:
time: 241 us; the launch traced here: 240 us
  waiting for transfers between devices  112 us (46%)
  starting transfers between devices  57.6 us (24%)
  matrix products  34.4 us (14%)
  local copies, waits for them, and re-layouts  17.8 us (7%)
  other arithmetic  16.6 us (7%)
    all_to_all x5, waiting for transfers between devices, exchange(): return lax.all_to_all(tiles, axis, split_axis=0, concat_axis=0, tiled=True)  59.7 us
    all_to_all x5, waiting for transfers between devices, spread(): return lax.all_to_all(tiles, axis, split_axis=0, concat_axis=0, tiled=True)  52.4 us
    dot_general x18, matrix products, dot(): return lax.dot_general(a, b, (dims, ((), ())), preferred_element_type=F32)  34.4 us
    all_to_all x5, starting transfers between devices, spread(): return lax.all_to_all(tiles, axis, split_axis=0, concat_axis=0, tiled=True)  30.6 us
    all_to_all x5, starting transfers between devices, exchange(): return lax.all_to_all(tiles, axis, split_axis=0, concat_axis=0, tiled=True)  27 us
    broadcast_in_dim x5, local copies, waits for them, and re-layouts, spread(): tiles = jnp.broadcast_to(block[None], (size, *block.shape))  5.21 us
  transfers between devices with their start and end apart: 10, of which 10 were waited for; matrix products, arithmetic and copies ran while one was open for 18% of the time, Pallas kernels for 0%

profile of v1, /device:TPU:1, one launch (start us, length us, event | category | flops | bytes accessed | tf_op | source)
XLA Modules:
  0.0 239.6 jit_solution(13872568873936279096)
XLA Ops:
  0.6 0.8 pad_maximum_fusion.2
  1.5 0.7 broadcast_in_dim.94
  2.2 6.0 %all-to-all-start = ((bf16[4,128,165]{1,2,0:T(8,128)(2,1)}), bf16[4,128,165]{1,2,0:T(8,128)(2,1)S(1)}, u32[]{:S(2)}, u32[]{:S(2)}) async-start(bf16[4,128,165]{1,2,0:T(8,128)(2,1)} %broadcast_in_dim.94), calls=%async_computation | async-start | bytes 344064 | tf_op jit(solution)/shard_map/all_to_all | solution.py:20
  8.2 5.4 %all-to-all-done = bf16[4,128,165]{1,2,0:T(8,128)(2,1)S(1)} async-done(((bf16[4,128,165]{1,2,0:T(8,128)(2,1)}), bf16[4,128,165]{1,2,0:T(8,128)(2,1)S(1)}, u32[]{:S(2)}, u32[]{:S(2)}) %all-to-all-start) | async-done | bytes 168992 | tf_op jit(solution)/shard_map/all_to_all | solution.py:20
  13.6 1.3 broadcast_in_dim.96
  14.9 8.4 %all-to-all-start.3 = ((bf16[32,128,165]{1,2,0:T(8,128)(2,1)}), bf16[32,128,165]{1,2,0:T(8,128)(2,1)}, u32[]{:S(2)}, u32[]{:S(2)}) async-start(bf16[32,128,165]{1,2,0:T(8,128)(2,1)} %broadcast_in_dim.96), calls=%async_computation.3 | async-start | bytes 2752512 | tf_op jit(solution)/shard_map/all_to_all | solution.py:20
  23.4 2.7 %multiply_reduce_fusion = f32[256]{0:T(256)S(1)} fusion(bf16[256,5280]{0,1:T(8,128)(2,1)S(1)} %copy-done, bf16[256,5280]{0,1:T(8,128)(2,1)} %param.8), kind=kLoop, calls=%fused_computation.2 | loop fusion | flops 6758144 | bytes 5407744 | tf_op jit(solution)/shard_map/reduce_sum | solution.py:70
  26.2 0.1 copy.30
  26.5 0.1 copy.31
  26.7 0.5 copy-done.6
  27.2 0.6 concatenate.24
  27.9 0.7 convolution_convert_fusion.1
  28.6 1.7 copy.34
  30.3 13.1 %all-to-all-done.3 = bf16[32,128,165]{1,2,0:T(8,128)(2,1)} async-done(((bf16[32,128,165]{1,2,0:T(8,128)(2,1)}), bf16[32,128,165]{1,2,0:T(8,128)(2,1)}, u32[]{:S(2)}, u32[]{:S(2)}) %all-to-all-start.3) | async-done | bytes 1351712 | tf_op jit(solution)/shard_map/all_to_all | solution.py:20
  43.3 5.7 %all-to-all-start.1 = ((bf16[32,8,2752]{2,1,0:T(8,128)(2,1)}), bf16[32,8,2752]{2,1,0:T(8,128)(2,1)}, u32[]{:S(2)}, u32[]{:S(2)}) async-start(bf16[32,8,2752]{2,1,0:T(8,128)(2,1)} %bitcast.6), calls=%async_computation.1 | async-start | bytes 2883584 | tf_op jit(solution)/shard_map/all_to_all | solution.py:24
  49.0 3.4 %multiply_convert_fusion = bf16[256,5280]{0,1:T(8,128)(2,1)S(1)} fusion(bf16[256,5280]{0,1:T(8,128)(2,1)} %param.9, bf16[256,5280]{0,1:T(8,128)(2,1)} %param.8, f32[256]{0:T(256)S(1)} %get-tuple-element.21), kind=kLoop, calls=%fused_computation.1 | loop fusion | flops 6758400 | bytes 8111104 | tf_op jit(solution)/shard_map/convert_element_type | solution.py:74
  52.4 2.4 %reshape.130 = bf16[128,5280]{0,1:T(8,128)(2,1)} reshape(bf16[128,32,165]{0,2,1:T(8,128)(2,1)} %bitcast.8) | data formatting | bytes 2703360 | tf_op jit(solution)/shard_map/reshape | solution.py:61
  54.8 2.0 fusion.51
  56.8 13.0 %all-to-all-done.1 = bf16[32,8,2752]{2,1,0:T(8,128)(2,1)} async-done(((bf16[32,8,2752]{2,1,0:T(8,128)(2,1)}), bf16[32,8,2752]{2,1,0:T(8,128)(2,1)}, u32[]{:S(2)}, u32[]{:S(2)}) %all-to-all-start.1) | async-done | bytes 1409056 | tf_op jit(solution)/shard_map/all_to_all | solution.py:24
  69.8 0.8 broadcast_in_dim.97
  70.6 6.1 %all-to-all-start.4 = ((f32[4,128,256]{2,1,0:T(8,128)}), f32[4,128,256]{2,1,0:T(8,128)S(1)}, u32[]{:S(2)}, u32[]{:S(2)}) async-start(f32[4,128,256]{2,1,0:T(8,128)} %broadcast_in_dim.97), calls=%async_computation.4 | async-start | bytes 1048576 | tf_op jit(solution)/shard_map/all_to_all | solution.py:20
  76.7 1.6 reduce_sum.96
  78.3 7.8 %all-to-all-done.4 = f32[4,128,256]{2,1,0:T(8,128)S(1)} async-done(((f32[4,128,256]{2,1,0:T(8,128)}), f32[4,128,256]{2,1,0:T(8,128)S(1)}, u32[]{:S(2)}, u32[]{:S(2)}) %all-to-all-start.4) | async-done | bytes 524320 | tf_op jit(solution)/shard_map/all_to_all | solution.py:20
  86.1 1.3 broadcast_in_dim.95
  87.4 4.7 %all-to-all-start.2 = ((bf16[32,8,2752]{2,1,0:T(8,128)(2,1)}), bf16[32,8,2752]{2,1,0:T(8,128)(2,1)}, u32[]{:S(2)}, u32[]{:S(2)}) async-start(bf16[32,8,2752]{2,1,0:T(8,128)(2,1)} %broadcast_in_dim.95), calls=%async_computation.2 | async-start | bytes 2883584 | tf_op jit(solution)/shard_map/all_to_all | solution.py:20
  92.1 13.1 %multiply_convert_fusion.1 = bf16[2240,256]{1,0:T(8,128)(2,1)} fusion(bf16[5280,2240]{0,1:T(8,128)(2,1)} %param.10, bf16[256,5280]{0,1:T(8,128)(2,1)S(1)} %multiply_convert_fusion), kind=kOutput, calls=%fused_computation.9 | convolution fusion | flops 6058393600 | bytes 27504640 | tf_op jit(solution)/shard_map/dot_general | solution.py:14
  105.2 7.7 %all-to-all-done.2 = bf16[32,8,2752]{2,1,0:T(8,128)(2,1)} async-done(((bf16[32,8,2752]{2,1,0:T(8,128)(2,1)}), bf16[32,8,2752]{2,1,0:T(8,128)(2,1)}, u32[]{:S(2)}, u32[]{:S(2)}) %all-to-all-start.2) | async-done | bytes 1409056 | tf_op jit(solution)/shard_map/all_to_all | solution.py:20
  112.9 2.1 fusion.3
  115.0 1.1 broadcast_in_dim.104
  116.1 6.6 %all-to-all-start.5 = ((f32[4,256,256]{2,1,0:T(8,128)}), f32[4,256,256]{2,1,0:T(8,128)}, u32[]{:S(2)}, u32[]{:S(2)}) async-start(f32[4,256,256]{2,1,0:T(8,128)} %broadcast_in_dim.104), calls=%async_computation.5 | async-start | bytes 2097152 | tf_op jit(solution)/shard_map/all_to_all | solution.py:24
  122.7 0.9 fusion.47
  123.6 2.0 fusion.10
  125.6 2.0 convolution_add_fusion.1
  127.6 10.2 %all-to-all-done.5 = f32[4,256,256]{2,1,0:T(8,128)} async-done(((f32[4,256,256]{2,1,0:T(8,128)}), f32[4,256,256]{2,1,0:T(8,128)}, u32[]{:S(2)}, u32[]{:S(2)}) %all-to-all-start.5) | async-done | bytes 1048608 | tf_op jit(solution)/shard_map/all_to_all | solution.py:24
  137.8 2.0 reduce_sum.101
  139.8 2.4 multiply_convert_fusion.2
  142.2 1.5 fusion
  143.7 0.2 convolution_multiply_fusion.1
  143.9 0.2 convolution_convert_fusion.3
  144.1 0.2 convolution_convert_fusion.2
  144.3 2.4 %copy.37 = bf16[256,2240]{1,0:T(8,128)(2,1)} copy(bf16[256,2240]{0,1:T(8,128)(2,1)} %fusion) | data formatting | bytes 2293760 | tf_op jit(solution)/shard_map/convert.8
  146.7 1.0 fusion.9
  147.7 0.1 concatenate.28
  147.9 2.5 %pad_maximum_fusion = bf16[32,8,2432]{2,1,0:T(8,128)(2,1)} fusion(bf16[32,8,192]{2,1,0:T(8,128)(2,1)S(1)} %concatenate.28, bf16[32,8,2240]{2,1,0:T(8,128)(2,1)} %bitcast.59), kind=kLoop, calls=%fused_computation.10 | loop fusion | flops 2490368 | bytes 2490368 | tf_op jit(solution)/shard_map/concatenate | solution.py:131
  150.3 4.7 %all-to-all-start.7 = ((bf16[32,8,2432]{2,1,0:T(8,128)(2,1)}), bf16[32,8,2432]{2,1,0:T(8,128)(2,1)}, u32[]{:S(2)}, u32[]{:S(2)}) async-start(bf16[32,8,2432]{2,1,0:T(8,128)(2,1)} %pad_maximum_fusion), calls=%async_computation.7 | async-start | bytes 2490368 | tf_op jit(solution)/shard_map/all_to_all | solution.py:24
  155.0 1.2 fusion.13
  156.1 1.0 fusion.22
  157.1 1.9 convolution_convert_fusion
  159.1 2.4 %reshape.133 = bf16[128,32,165]{0,2,1:T(8,128)(2,1)} reshape(bf16[128,5280]{0,1:T(8,128)(2,1)} %convolution_convert_fusion) | data formatting | bytes 2703360 | tf_op jit(solution)/shard_map/reshape | solution.py:121
  161.5 12.3 %all-to-all-done.7 = bf16[32,8,2432]{2,1,0:T(8,128)(2,1)} async-done(((bf16[32,8,2432]{2,1,0:T(8,128)(2,1)}), bf16[32,8,2432]{2,1,0:T(8,128)(2,1)}, u32[]{:S(2)}, u32[]{:S(2)}) %all-to-all-start.7) | async-done | bytes 1245216 | tf_op jit(solution)/shard_map/all_to_all | solution.py:24
  173.8 4.8 %all-to-all-start.6 = ((bf16[32,128,165]{1,2,0:T(8,128)(2,1)}), bf16[32,128,165]{1,2,0:T(8,128)(2,1)S(1)}, u32[]{:S(2)}, u32[]{:S(2)}) async-start(bf16[32,128,165]{1,2,0:T(8,128)(2,1)} %bitcast.12), calls=%async_computation.6 | async-start | bytes 2752512 | tf_op jit(solution)/shard_map/all_to_all | solution.py:24
  178.6 1.5 reduce_sum.104
  180.1 18.6 %all-to-all-done.6 = bf16[32,128,165]{1,2,0:T(8,128)(2,1)S(1)} async-done(((bf16[32,128,165]{1,2,0:T(8,128)(2,1)}), bf16[32,128,165]{1,2,0:T(8,128)(2,1)S(1)}, u32[]{:S(2)}, u32[]{:S(2)}) %all-to-all-start.6) | async-done | bytes 1351712 | tf_op jit(solution)/shard_map/all_to_all | solution.py:24
  198.7 1.1 broadcast_in_dim.106
  199.8 5.5 %all-to-all-start.8 = ((bf16[32,8,2432]{2,1,0:T(8,128)(2,1)}), bf16[32,8,2432]{2,1,0:T(8,128)(2,1)S(1)}, u32[]{:S(2)}, u32[]{:S(2)}) async-start(bf16[32,8,2432]{2,1,0:T(8,128)(2,1)} %broadcast_in_dim.106), calls=%async_computation.8 | async-start | bytes 2490368 | tf_op jit(solution)/shard_map/all_to_all | solution.py:20
  205.3 0.2 convert_reduce_fusion
  205.8 18.5 %all-to-all-done.8 = bf16[32,8,2432]{2,1,0:T(8,128)(2,1)S(1)} async-done(((bf16[32,8,2432]{2,1,0:T(8,128)(2,1)}), bf16[32,8,2432]{2,1,0:T(8,128)(2,1)S(1)}, u32[]{:S(2)}, u32[]{:S(2)}) %all-to-all-start.8) | async-done | bytes 1245216 | tf_op jit(solution)/shard_map/all_to_all | solution.py:20
  224.4 2.3 fusion.1
  226.7 0.2 reshape.135
  226.9 5.3 %all-to-all-start.9 = ((f32[4,64,165]{2,1,0:T(8,128)}), f32[4,64,165]{2,1,0:T(8,128)S(1)}, u32[]{:S(2)}, u32[]{:S(2)}) async-start(f32[4,64,165]{2,1,0:T(8,128)} %bitcast.16), calls=%async_computation.9 | async-start | bytes 524288 | tf_op jit(solution)/shard_map/all_to_all | solution.py:24
  232.2 0.1 convolution_add_fusion.3
  232.3 0.8 fusion.8
  233.1 5.6 %all-to-all-done.9 = f32[4,64,165]{2,1,0:T(8,128)S(1)} async-done(((f32[4,64,165]{2,1,0:T(8,128)}), f32[4,64,165]{2,1,0:T(8,128)S(1)}, u32[]{:S(2)}, u32[]{:S(2)}) %all-to-all-start.9) | async-done | bytes 168992 | tf_op jit(solution)/shard_map/all_to_all | solution.py:24
  238.8 0.8 fusion.7
  (35 shorter events, 1.0 us)
Async XLA Ops:
  2.2 11.3 %all-to-all-start = ((bf16[4,128,165]{1,2,0:T(8,128)(2,1)}), bf16[4,128,165]{1,2,0:T(8,128)(2,1)S(1)}, u32[]{:S(2)}, u32[]{:S(2)}) async-start(bf16[4,128,165]{1,2,0:T(8,128)(2,1)} %broadcast_in_dim.94), calls=%async_computation | async-start | bytes 344064 | tf_op jit(solution)/shard_map/all_to_all | solution.py:20
  14.8 8.4 %copy-start.7 = (s32[8]{0:T(128)S(1)}, s32[8]{0:T(128)}, u32[]{:S(2)}) copy-start(s32[8]{0:T(128)} %param.15) | copy-start | bytes 100
  14.8 8.4 %copy-start.8 = (s32[8]{0:T(128)S(1)}, s32[8]{0:T(128)}, u32[]{:S(2)}) copy-start(s32[8]{0:T(128)} %param.14) | copy-start | bytes 100
  14.8 8.5 %copy-start = (bf16[256,5280]{0,1:T(8,128)(2,1)S(1)}, bf16[256,5280]{0,1:T(8,128)(2,1)}, u32[]{:S(2)}) copy-start(bf16[256,5280]{0,1:T(8,128)(2,1)} %param.9) | copy-start | bytes 8110084
  14.9 28.5 %all-to-all-start.3 = ((bf16[32,128,165]{1,2,0:T(8,128)(2,1)}), bf16[32,128,165]{1,2,0:T(8,128)(2,1)}, u32[]{:S(2)}, u32[]{:S(2)}) async-start(bf16[32,128,165]{1,2,0:T(8,128)(2,1)} %broadcast_in_dim.96), calls=%async_computation.3 | async-start | bytes 2752512 | tf_op jit(solution)/shard_map/all_to_all | solution.py:20
  26.1 1.1 copy-start.6
  26.6 1.3 copy-start.3
  43.3 26.5 %all-to-all-start.1 = ((bf16[32,8,2752]{2,1,0:T(8,128)(2,1)}), bf16[32,8,2752]{2,1,0:T(8,128)(2,1)}, u32[]{:S(2)}, u32[]{:S(2)}) async-start(bf16[32,8,2752]{2,1,0:T(8,128)(2,1)} %bitcast.6), calls=%async_computation.1 | async-start | bytes 2883584 | tf_op jit(solution)/shard_map/all_to_all | solution.py:24
  70.6 15.5 %all-to-all-start.4 = ((f32[4,128,256]{2,1,0:T(8,128)}), f32[4,128,256]{2,1,0:T(8,128)S(1)}, u32[]{:S(2)}, u32[]{:S(2)}) async-start(f32[4,128,256]{2,1,0:T(8,128)} %broadcast_in_dim.97), calls=%async_computation.4 | async-start | bytes 1048576 | tf_op jit(solution)/shard_map/all_to_all | solution.py:20
  86.1 1.3 copy-start.1
  87.4 25.6 %all-to-all-start.2 = ((bf16[32,8,2752]{2,1,0:T(8,128)(2,1)}), bf16[32,8,2752]{2,1,0:T(8,128)(2,1)}, u32[]{:S(2)}, u32[]{:S(2)}) async-start(bf16[32,8,2752]{2,1,0:T(8,128)(2,1)} %broadcast_in_dim.95), calls=%async_computation.2 | async-start | bytes 2883584 | tf_op jit(solution)/shard_map/all_to_all | solution.py:20
  92.1 13.1 %copy-start.2 = (f32[4,128,256]{2,1,0:T(8,128)S(1)}, f32[4,128,256]{2,1,0:T(8,128)}, u32[]{:S(2)}) copy-start(f32[4,128,256]{2,1,0:T(8,128)} %copy-done.1) | copy-start | bytes 1572868
  116.1 21.7 %all-to-all-start.5 = ((f32[4,256,256]{2,1,0:T(8,128)}), f32[4,256,256]{2,1,0:T(8,128)}, u32[]{:S(2)}, u32[]{:S(2)}) async-start(f32[4,256,256]{2,1,0:T(8,128)} %broadcast_in_dim.104), calls=%async_computation.5 | async-start | bytes 2097152 | tf_op jit(solution)/shard_map/all_to_all | solution.py:24
  139.8 2.4 copy-start.5
  150.3 23.5 %all-to-all-start.7 = ((bf16[32,8,2432]{2,1,0:T(8,128)(2,1)}), bf16[32,8,2432]{2,1,0:T(8,128)(2,1)}, u32[]{:S(2)}, u32[]{:S(2)}) async-start(bf16[32,8,2432]{2,1,0:T(8,128)(2,1)} %pad_maximum_fusion), calls=%async_computation.7 | async-start | bytes 2490368 | tf_op jit(solution)/shard_map/all_to_all | solution.py:24
  173.8 24.9 %all-to-all-start.6 = ((bf16[32,128,165]{1,2,0:T(8,128)(2,1)}), bf16[32,128,165]{1,2,0:T(8,128)(2,1)S(1)}, u32[]{:S(2)}, u32[]{:S(2)}) async-start(bf16[32,128,165]{1,2,0:T(8,128)(2,1)} %bitcast.12), calls=%async_computation.6 | async-start | bytes 2752512 | tf_op jit(solution)/shard_map/all_to_all | solution.py:24
  199.8 24.4 %all-to-all-start.8 = ((bf16[32,8,2432]{2,1,0:T(8,128)(2,1)}), bf16[32,8,2432]{2,1,0:T(8,128)(2,1)S(1)}, u32[]{:S(2)}, u32[]{:S(2)}) async-start(bf16[32,8,2432]{2,1,0:T(8,128)(2,1)} %broadcast_in_dim.106), calls=%async_computation.8 | async-start | bytes 2490368 | tf_op jit(solution)/shard_map/all_to_all | solution.py:20
  226.7 12.1 %copy-start.4 = (bf16[4,64,165]{2,1,0:T(8,128)(2,1)S(1)}, bf16[4,64,165]{2,1,0:T(8,128)(2,1)}, u32[]{:S(2)}) copy-start(bf16[4,64,165]{2,1,0:T(8,128)(2,1)} %copy-done.3) | copy-start | bytes 253444
  226.9 11.9 %all-to-all-start.9 = ((f32[4,64,165]{2,1,0:T(8,128)}), f32[4,64,165]{2,1,0:T(8,128)S(1)}, u32[]{:S(2)}, u32[]{:S(2)}) async-start(f32[4,64,165]{2,1,0:T(8,128)} %bitcast.16), calls=%async_computation.9 | async-start | bytes 524288 | tf_op jit(solution)/shard_map/all_to_all | solution.py:24

commit v2 on v1

v2 whole, which is shorter than its diff:
```python
import functools

import jax
import jax.numpy as jnp
from jax import lax
from jax.experimental import pallas as pl
from jax.experimental.pallas import tpu as pltpu
from jax.sharding import PartitionSpec as P

LENGTH = 1024
epsilon = 1e-06
loss_scale = 64.0
F32 = jnp.float32
BF16 = jnp.bfloat16
MESH = pl.DeviceIdType.MESH
NN = ((1,), (0,))
NT = ((1,), (1,))
TN = ((0,), (0,))
ROWS = 320
TILE = 128


def dot(a, b, dims=NN):
    return lax.dot_general(a, b, (dims, ((), ())), preferred_element_type=F32)


def silu_slope(logits):
    sigmoid = jax.nn.sigmoid(logits)
    return sigmoid * (1.0 + logits * (1.0 - sigmoid))


def ceil_to(value, multiple):
    return -(-value // multiple) * multiple


def kernel(
    n_tp,
    n_grp,
    sizes,
    state_hbm,
    inject_hbm,
    up_hbm,
    down_hbm,
    tall_ref,
    pair_ref,
    flag_ref,
    direct_ref,
    rest_ref,
    state_v,
    inject_v,
    up_v,
    down_v,
    summed_v,
    normed_v,
    blocks_v,
    hidden_v,
    pairs_v,
    tall_v,
    m_send,
    m_recv,
    m_full,
    g_send,
    g_recv,
    g_full,
    c_send,
    c_recv,
    c_full,
    f_send,
    f_recv,
    z_all,
    small_all,
    term_all,
    term_own,
    out_send,
    out_recv,
    keep,
    load_sem,
    up_sem,
    send_sem,
    recv_sem,
):
    tokens, width, cols, own, hidden, wide, scale = sizes
    units = own * n_tp
    tall = tall_ref.shape[0]
    me_g = lax.axis_index("grp")
    me_t = lax.axis_index("tp")

    def over_grp(slot, source, target):
        def step(k, carry):
            peer = lax.rem(me_g + k, n_grp)
            pltpu.make_async_remote_copy(
                src_ref=source(peer),
                dst_ref=target(k),
                send_sem=send_sem.at[slot],
                recv_sem=recv_sem.at[slot],
                device_id={"grp": peer},
                device_id_type=MESH,
            ).start()
            return carry

        lax.fori_loop(1, n_grp, step, 0)

    def over_tp(slot, source, target):
        for k in range(1, n_tp):
            peer = lax.rem(me_t + k, n_tp)
            pltpu.make_async_remote_copy(
                src_ref=source(peer),
                dst_ref=target(k),
                send_sem=send_sem.at[slot],
                recv_sem=recv_sem.at[slot],
                device_id={"tp": peer},
                device_id_type=MESH,
            ).start()

    def arrived(slot, buffer):
        part = buffer.at[pl.ds(0, buffer.shape[0] - 1)]
        pltpu.make_async_copy(part, part, recv_sem.at[slot]).wait()

    def sent(slot, buffer):
        part = buffer.at[pl.ds(0, buffer.shape[0] - 1)]
        pltpu.make_async_copy(part, part, send_sem.at[slot]).wait()

    def summed_slots(first, recv):
        def add(k, total):
            return total + recv[k].astype(F32)

        return lax.fori_loop(1, n_grp, add, first.astype(F32))

    barrier = pltpu.get_barrier_semaphore()

    def greet(k, carry):
        pl.semaphore_signal(
            barrier, inc=1, device_id={"grp": lax.rem(me_g + k, n_grp)}, device_id_type=MESH
        )
        return carry

    lax.fori_loop(1, n_grp, greet, 0)
    for k in range(1, n_tp):
        pl.semaphore_signal(
            barrier, inc=1, device_id={"tp": lax.rem(me_t + k, n_tp)}, device_id_type=MESH
        )
    load_state = pltpu.make_async_copy(state_hbm, state_v, load_sem.at[0])
    load_inject = pltpu.make_async_copy(inject_hbm, inject_v, load_sem.at[1])
    load_down = pltpu.make_async_copy(down_hbm, down_v, load_sem.at[2])
    load_state.start()
    load_inject.start()
    load_down.start()

    def up_copy(i):
        rows = pl.ds(pl.multiple_of(i * ROWS, ROWS), ROWS)
        return pltpu.make_async_copy(up_hbm.at[rows], up_v.at[rows], up_sem.at[i])

    chunks = hidden // ROWS
    for i in range(chunks):
        up_copy(i).start()
    pl.semaphore_wait(barrier, n_grp - 1 + n_tp - 1)

    over_tp(0, lambda p: pair_ref, lambda k: pairs_v.at[me_t])
    over_grp(1, lambda p: tall_ref, lambda k: tall_v.at[me_g])
    pairs_v[me_t] = pair_ref[...]
    tall_v[me_g] = tall_ref[...]

    load_state.wait()
    load_inject.wait()
    step_rows = 160

    def add_rows(i, square):
        rows = pl.ds(pl.multiple_of(i * step_rows, step_rows), step_rows)
        value = state_v[rows].astype(F32) + inject_v[rows].astype(F32)
        summed_v[rows] = value
        return square + (value * value).reshape(step_rows // 8, 8, tokens).sum(axis=0)

    square = lax.fori_loop(0, width // step_rows, add_rows, jnp.zeros((8, tokens), F32))
    summed_v[pl.ds(width, 16)] = jnp.zeros((16, tokens), F32)
    square = square.sum(axis=0, keepdims=True)
    mean1 = square / width + epsilon
    rho1 = lax.rsqrt(mean1)
    norm1 = jnp.sqrt(mean1)

    def scale_rows(i, carry):
        rows = pl.ds(pl.multiple_of(i * step_rows, step_rows), step_rows)
        normed_v[rows] = (summed_v[rows] * rho1).astype(BF16)
        return carry

    lax.fori_loop(0, width // step_rows, scale_rows, 0)

    def block_rows(i, carry):
        for part in range(8):
            base = pl.multiple_of(i * (8 * cols) + part * cols // 8 * 8, 8)
            value = summed_v[pl.ds(base, tall + 8)]
            shift = part * cols % 8
            blocks_v[i * 8 + part] = (value[shift : shift + tall] * rho1).astype(BF16)
        return carry

    lax.fori_loop(0, n_grp // 8, block_rows, 0)

    arrived(0, pairs_v)
    load_down.wait()
    up_cols = pairs_v[:, :own].reshape(units, cols)
    down_cols = pairs_v[:, own:].reshape(units, cols)
    own_down = pair_ref[own:]
    spans = [(c, min(640, hidden - c)) for c in range(0, hidden, 640)]
    for c, w in spans:
        m_send[:, :, c : c + w] = dot(down_cols, down_v[:, c : c + w]).reshape(n_grp, 8, w).astype(BF16)
    if wide > hidden:
        m_send[:, :, hidden:wide] = jnp.zeros((n_grp, 8, wide - hidden), BF16)
    grams = jnp.concatenate([dot(own_down, down_cols, NT), dot(own_down, up_cols, NT)], axis=0)
    half = n_grp // 2
    m_send[:half, :, wide:] = grams[:, :TILE].reshape(half, 8, TILE).astype(BF16)
    m_send[half:, :, wide:] = grams[:, TILE:].reshape(half, 8, TILE).astype(BF16)
    over_grp(2, lambda p: m_send.at[p], lambda k: m_recv.at[k])

    def up_rows(i, carry):
        up_copy(i).wait()
        rows = pl.ds(pl.multiple_of(i * ROWS, ROWS), ROWS)
        hidden_v[rows] = jax.nn.silu(dot(up_v[rows], normed_v[...])).astype(BF16)
        return carry

    lax.fori_loop(0, chunks, up_rows, 0)

    arrived(1, tall_v)
    group = 4

    def logit_rows(j, total):
        a = tall_v[pl.ds(j * group, group)].reshape(group * tall, 2 * own)
        b = blocks_v[pl.ds(j * group, group)].reshape(group * tall, tokens)
        return total + dot(a, b, TN)

    z_all[me_t] = lax.fori_loop(0, n_grp // group, logit_rows, jnp.zeros((2 * own, tokens), F32))
    over_tp(3, lambda p: z_all.at[me_t], lambda k: z_all.at[me_t])

    arrived(2, m_recv)
    m_full[me_g] = summed_slots(m_send[me_g], m_recv).astype(BF16)
    over_grp(4, lambda p: m_full.at[me_g], lambda k: m_full.at[me_g])
    arrived(4, m_full)

    low = m_full[:half, :, wide:].reshape(2 * own, TILE)
    high = m_full[half:, :, wide:].reshape(2 * own, TILE)
    small_all[me_t] = jnp.concatenate([low, high], axis=1)
    over_tp(5, lambda p: small_all.at[me_t], lambda k: small_all.at[me_t])
    teach = m_full[:, :, :hidden].reshape(units, hidden)
    term = dot(teach, hidden_v[...])
    term_own[...] = term.astype(BF16)
    over_tp(6, lambda p: term_own, lambda k: term_all.at[k])

    arrived(3, z_all)
    arrived(5, small_all)
    gram = small_all[:, :own].reshape(units, units)
    cross = small_all[:, own:].reshape(units, units)
    logits1 = z_all[:, :own].reshape(units, tokens)
    along = z_all[:, own:].reshape(units, tokens) * norm1
    upward = logits1 * norm1
    taught = flag_ref[0:1]
    deep = flag_ref[1:2]
    hidden1 = jax.nn.silu(logits1).astype(BF16)
    gram1 = dot(gram, hidden1)
    hidden1_f = hidden1.astype(F32)
    moved = along + gram1
    square2 = square + jnp.sum(hidden1_f * (along + moved), axis=0, keepdims=True)
    rho2 = lax.rsqrt(jnp.maximum(square2, 0.0) / width + epsilon)
    upward2 = upward + dot(cross, hidden1, TN)
    logits2 = upward2 * rho2
    hidden2 = (jax.nn.silu(logits2) * deep).astype(BF16)
    total_f = hidden1_f + hidden2.astype(F32)
    total = total_f.astype(BF16)
    taught_total = (total_f * taught).astype(BF16)
    for c, w in spans:
        part = dot(taught_total, hidden_v[c : c + w], NT) * (-scale)
        g_send[:, :, c : c + w] = part.reshape(n_grp, 8, w).astype(BF16)
    over_grp(7, lambda p: g_send.at[p], lambda k: g_recv.at[k])

    arrived(6, term_all)
    for k in range(1, n_tp):
        term = term + term_all[k].astype(F32)
    slope = scale * (gram1 + dot(gram, hidden2) - term * taught)
    q2 = slope * silu_slope(logits2) * deep
    mu = jnp.sum(upward2 * q2, axis=0, keepdims=True) / width
    rq2 = (rho2 * q2).astype(BF16)
    ratio = rho2 * rho2 * rho2 * mu
    slope1 = slope + dot(cross, rq2) - ratio * moved
    q1 = slope1 * silu_slope(logits1)
    rq2_f = rq2.astype(F32)
    keep[0] = q1 + rq2_f * norm1
    keep[1] = -hidden1_f * (ratio * norm1)
    keep[2] = total_f
    keep[3] = hidden1_f * ratio
    keep[4] = hidden1_f
    keep[5] = rq2_f
    mine = pl.ds(pl.multiple_of(me_t * own, own), own)
    left = jnp.concatenate([keep[0, mine], keep[1, mine]], axis=0).astype(BF16)

    def direct_rows(j, carry):
        b = blocks_v[pl.ds(j * group, group)].reshape(group * tall, tokens)
        f_send[pl.ds(j * group, group)] = dot(b, left, NT).reshape(group, tall, 2 * own).astype(BF16)
        return carry

    lax.fori_loop(0, n_grp // group, direct_rows, 0)
    c1 = scale * dot(keep[2, mine].astype(BF16), total, NT) - dot(keep[3, mine].astype(BF16), hidden1, NT)
    c2 = dot(keep[4, mine].astype(BF16), rq2, NT)
    c3 = dot(keep[5, mine].astype(BF16), hidden1, NT)
    folded = jnp.concatenate([c1, c2, c3, jnp.zeros((own, units), F32)], axis=0)
    c_send[...] = folded.reshape(n_grp, 8, units).astype(BF16)
    over_grp(8, lambda p: c_send.at[p], lambda k: c_recv.at[k])
    over_grp(9, lambda p: f_send.at[p], lambda k: f_recv.at[k])

    arrived(7, g_recv)
    g_full[me_g] = summed_slots(g_send[me_g], g_recv).astype(BF16)
    over_grp(10, lambda p: g_full.at[me_g], lambda k: g_full.at[me_g])
    arrived(8, c_recv)
    c_full[me_g] = summed_slots(c_send[me_g], c_recv).astype(BF16)
    over_grp(11, lambda p: c_full.at[me_g], lambda k: c_full.at[me_g])
    arrived(9, f_recv)
    direct_ref[...] = summed_slots(f_send[me_g], f_recv)
    arrived(10, g_full)
    out_send[...] = dot(g_full[...].reshape(units, hidden), down_v[...], NT).reshape(n_tp, own, cols)
    over_tp(12, lambda p: out_send.at[p], lambda k: out_recv.at[k])
    arrived(11, c_full)
    folded = c_full[...].reshape(units, units)
    up_cols = pairs_v[:, :own].reshape(units, cols)
    down_cols = pairs_v[:, own:].reshape(units, cols)
    down_rest = dot(folded[:own], down_cols) + dot(folded[own : 2 * own], up_cols)
    rest_ref[:own] = dot(folded[2 * own : 3 * own], down_cols)
    arrived(12, out_recv)
    down_rest = down_rest + out_send[me_t]
    for k in range(1, n_tp):
        down_rest = down_rest + out_recv[k]
    rest_ref[own:] = down_rest

    sent(0, pairs_v)
    sent(1, tall_v)
    sent(2, m_recv)
    sent(3, z_all)
    sent(4, m_full)
    sent(5, small_all)
    sent(6, term_all)
    sent(7, g_recv)
    sent(8, c_recv)
    sent(9, f_recv)
    sent(10, g_full)
    sent(11, c_full)
    sent(12, out_recv)


def body(
    teacher_state,
    injection,
    teacher_up,
    teacher_down,
    student_up,
    student_down,
    teacher_step,
    student_depth,
):
    n_tp, n_grp = lax.axis_size("tp"), lax.axis_size("grp")
    tokens, width = teacher_state.shape
    cols, own = student_up.shape
    units = own * n_tp
    hidden = teacher_down.shape[0]
    scale = loss_scale * 2.0 / (tokens * n_grp)
    tall = ceil_to(cols, 16)
    wide = ceil_to(hidden, TILE)

    pair = jnp.concatenate([student_up.T, student_down], axis=0)
    tall_pair = jnp.pad(pair.T, ((0, tall - cols), (0, 0)))
    sequence = lax.axis_index("grp") * tokens // LENGTH
    here = jnp.arange(teacher_step.shape[0], dtype=jnp.int32) == sequence
    taught = jnp.sum(jnp.where(here & (teacher_step == 1), 1.0, 0.0))
    deep = jnp.sum(jnp.where(here & (student_depth == 2), 1.0, 0.0))
    flags = jnp.where(jnp.arange(8)[:, None] == 0, taught, deep) + jnp.zeros((8, tokens), F32)

    any_spec = pl.BlockSpec(memory_space=pl.ANY)
    vmem = pl.BlockSpec(memory_space=pltpu.VMEM)
    chunk = (n_grp, 8, hidden)
    direct, rest = pl.pallas_call(
        functools.partial(kernel, n_tp, n_grp, (tokens, width, cols, own, hidden, wide, scale)),
        out_shape=(
            jax.ShapeDtypeStruct((tall, 2 * own), F32),
            jax.ShapeDtypeStruct((2 * own, cols), F32),
        ),
        in_specs=[any_spec] * 4 + [vmem] * 3,
        out_specs=(vmem, vmem),
        scratch_shapes=[
            pltpu.VMEM((width, tokens), BF16),
            pltpu.VMEM((width, tokens), BF16),
            pltpu.VMEM((hidden, width), BF16),
            pltpu.VMEM((cols, hidden), BF16),
            pltpu.VMEM((width + 16, tokens), F32),
            pltpu.VMEM((width, tokens), BF16),
            pltpu.VMEM((n_grp, tall, tokens), BF16),
            pltpu.VMEM((hidden, tokens), BF16),
            pltpu.VMEM((n_tp, 2 * own, cols), BF16),
            pltpu.VMEM((n_grp, tall, 2 * own), BF16),
            pltpu.VMEM((n_grp, 8, wide + TILE), BF16),
            pltpu.VMEM((n_grp, 8, wide + TILE), BF16),
            pltpu.VMEM((n_grp, 8, wide + TILE), BF16),
            pltpu.VMEM(chunk, BF16),
            pltpu.VMEM(chunk, BF16),
            pltpu.VMEM(chunk, BF16),
            pltpu.VMEM((n_grp, 8, units), BF16),
            pltpu.VMEM((n_grp, 8, units), BF16),
            pltpu.VMEM((n_grp, 8, units), BF16),
            pltpu.VMEM((n_grp, tall, 2 * own), BF16),
            pltpu.VMEM((n_grp, tall, 2 * own), BF16),
            pltpu.VMEM((n_tp, 2 * own, tokens), F32),
            pltpu.VMEM((n_tp, 2 * own, units), BF16),
            pltpu.VMEM((n_tp, units, tokens), BF16),
            pltpu.VMEM((units, tokens), BF16),
            pltpu.VMEM((n_tp, own, cols), F32),
            pltpu.VMEM((n_tp, own, cols), F32),
            pltpu.VMEM((6, units, tokens), F32),
            pltpu.SemaphoreType.DMA((3,)),
            pltpu.SemaphoreType.DMA((hidden // ROWS,)),
            pltpu.SemaphoreType.DMA((13,)),
            pltpu.SemaphoreType.DMA((13,)),
        ],
        compiler_params=pltpu.CompilerParams(
            collective_id=0, has_side_effects=True, vmem_limit_bytes=67043328
        ),
    )(teacher_state.T, injection.T, teacher_up.T, teacher_down.T, tall_pair, pair, flags)
    grad_up = direct[:cols, :own] + rest[:own].T
    grad_down = direct[:cols, own:].T + rest[own:]
    return (grad_up, grad_down)


def solution(mesh):
    in_specs = (
        P("grp", None),
        P("grp", None),
        P(None, "tp"),
        P("tp", "grp"),
        P("grp", "tp"),
        P("tp", "grp"),
        P(),
        P(),
    )
    out_specs = (P("grp", "tp"), P("tp", "grp"))
    return jax.shard_map(body, mesh=mesh, in_specs=in_specs, out_specs=out_specs, check_vma=False)
```

time: 241 us -> 150 us (0.62)
  the two profiles are of different devices: /device:TPU:1 before, /device:TPU:5 now
where the time goes in v2:
time: 150 us; the launch traced here: 149 us
  Pallas kernels  139 us (93%)
  other arithmetic  6.95 us (5%)
  local copies, waits for them, and re-layouts  2.39 us (2%)
    pallas_call x1, Pallas kernels, body(): pl.pallas_call(functools.partial(kernel, n_tp, n_grp, (tokens, width, col...  139 us

profile of v2, /device:TPU:5, one launch (start us, length us, event | category | flops | bytes accessed | tf_op | source)
XLA Modules:
  0.0 149.3 jit_solution(15710717081649516722)
XLA Ops:
  0.6 1.3 fusion.1
  1.9 1.3 compare_select_fusion
  3.2 0.7 add.14.flag_ref
  3.9 1.4 pad_maximum_fusion
  5.3 0.1 copy.13
  5.4 0.6 pad.4.clone.tall_ref
  6.1 139.3 %shard_map.95 = (f32[176,128]{1,0:T(8,128)}, f32[128,165]{1,0:T(8,128)}) custom-call(bf16[5280,256]{1,0:T(8,128)(2,1)} %bitcast.14, bf16[5280,256]{1,0:T(8,128)(2,1)} %bitcast.15, bf16[2240,5280]{1,0:T(8,128)(2,1)} %bitcast.13, bf16[165,2240]{1,0:T(8,128)(2,1)} %bitcast.16, bf16[176,128]{1,0:T(8,128)(2,1)} %pad.4.clone.tall_ref, ...), custom_call_target="tpu_custom_call" | custom-call | tf_op jit(solution)/shard_map/pallas_call | solution.py:374
  145.3 1.0 copy.11
  146.3 1.5 fusion
  147.8 1.5 slice_add_fusion

commit v3 on v2

v3 whole, which is shorter than its diff:
```python
import functools

import jax
import jax.numpy as jnp
from jax import lax
from jax.experimental import pallas as pl
from jax.experimental.pallas import tpu as pltpu
from jax.sharding import PartitionSpec as P

LENGTH = 1024
epsilon = 1e-06
loss_scale = 64.0
F32 = jnp.float32
BF16 = jnp.bfloat16
MESH = pl.DeviceIdType.MESH
NN = ((1,), (0,))
NT = ((1,), (1,))
TN = ((0,), (0,))
ROWS = 320
TILE = 128
GRID = (4, 4, 2)
GATHER_ORDERS = ((1, 2, 0), (2, 0, 1), (0, 1, 2))


def lane_cuts(*ends):
    starts = (0, *ends[:-1])
    return tuple((slice(None), pl.ds(a * TILE, (b - a) * TILE)) for a, b in zip(starts, ends))


def row_cuts(*ends):
    starts = (0, *ends[:-1])
    return tuple((pl.ds(a * 8, (b - a) * 8), slice(None)) for a, b in zip(starts, ends))


M_CUTS = lane_cuts(6, 12, 18)
F_CUTS = row_cuts(7, 14, 22)


def room_shapes(rows, lanes, cuts):
    rooms = []
    for order, (r, c) in zip(GATHER_ORDERS, cuts):
        tail = (rows if r == slice(None) else r.size, lanes if c == slice(None) else c.size)
        sizes = [GRID[a] for a in order]
        middle = tuple(GRID[a] for a in sorted(order[:2]))
        landing = (
            pltpu.VMEM((sizes[2] - 1, *middle, *tail), BF16),
            pltpu.VMEM((sizes[1] - 1, sizes[0], *tail), BF16),
            pltpu.VMEM((sizes[0] - 1, *tail), BF16),
        )
        held = (pltpu.VMEM((*middle, *tail), BF16), pltpu.VMEM((sizes[0], *tail), BF16))
        rooms.append((landing, held))
    return rooms


def dot(a, b, dims=NN):
    return lax.dot_general(a, b, (dims, ((), ())), preferred_element_type=F32)


def silu_slope(logits):
    sigmoid = jax.nn.sigmoid(logits)
    return sigmoid * (1.0 + logits * (1.0 - sigmoid))


def ceil_to(value, multiple):
    return -(-value // multiple) * multiple


def kernel(
    n_tp,
    n_grp,
    sizes,
    state_hbm,
    inject_hbm,
    up_hbm,
    down_hbm,
    tall_ref,
    pair_ref,
    step_ref,
    depth_ref,
    direct_ref,
    rest_ref,
    state_v,
    inject_v,
    up_v,
    down_v,
    summed_v,
    normed_v,
    blocks_v,
    hidden_v,
    pairs_v,
    tall_v,
    m_send,
    m_full,
    g_send,
    g_full,
    c_send,
    c_recv,
    c_full,
    k_send,
    k_recv,
    k_full,
    f_send,
    stages,
    z_all,
    small_all,
    term_f32,
    term_send,
    term_recv,
    half_send,
    half_recv,
    term_sum,
    out_part,
    out_pair,
    out_send,
    out_last,
    keep,
    load_sem,
    up_sem,
    send_sem,
    recv_sem,
    stage_send,
    stage_recv,
    tp_send,
    tp_recv,
):
    tokens, width, cols, own, hidden, wide, scale = sizes
    units = own * n_tp
    tall = tall_ref.shape[0]
    me_g = lax.axis_index("grp")
    me_t = lax.axis_index("tp")
    me = (me_g // (GRID[1] * GRID[2]), me_g // GRID[2] % GRID[1], me_g % GRID[2])

    def along_axis(axis, coord):
        z, x, y = (coord if a == axis else me[a] for a in range(3))
        return {"grp": (z * GRID[1] + x) * GRID[2] + y}

    def remote(source, target, slot, device):
        pltpu.make_async_remote_copy(
            src_ref=source,
            dst_ref=target,
            send_sem=stage_send.at[slot],
            recv_sem=stage_recv.at[slot],
            device_id=device,
            device_id_type=MESH,
        ).start()

    pending = []

    def wait_bytes(part, sem):
        pltpu.make_async_copy(part, part, sem).wait()

    def gather_start(slot, buffer, cuts, stage):
        for p, order in enumerate(GATHER_ORDERS):
            axis = order[stage]
            where = [me[a] for a in range(3)]
            for a in order[:stage]:
                where[a] = pl.ds(0, GRID[a])
            part = buffer.at[(*where, *cuts[p])]
            for k in range(1, GRID[axis]):
                peer = lax.rem(me[axis] + k, GRID[axis])
                remote(part, part, slot + 3 * p + stage, along_axis(axis, peer))
            where[axis] = pl.ds(0, GRID[axis] - 1)
            pending.append((buffer.at[(*where, *cuts[p])], stage_send.at[slot + 3 * p + stage]))

    def gather_wait(slot, buffer, cuts, stage):
        for p, order in enumerate(GATHER_ORDERS):
            axis = order[stage]
            where = [me[a] for a in range(3)]
            for a in order[:stage]:
                where[a] = pl.ds(0, GRID[a])
            where[axis] = pl.ds(0, GRID[axis] - 1)
            wait_bytes(buffer.at[(*where, *cuts[p])], stage_recv.at[slot + 3 * p + stage])

    def scatter_start(slot, buffer, rooms, cuts, stage):
        for p, order in enumerate(GATHER_ORDERS):
            axis = order[2 - stage]
            landing, held = rooms[p]
            for k in range(1, GRID[axis]):
                peer = lax.rem(me[axis] + k, GRID[axis])
                if stage == 0:
                    where = [pl.ds(0, GRID[a]) for a in range(3)]
                    where[axis] = peer
                    source = buffer.at[(*where, *cuts[p])]
                elif stage == 1:
                    source = held[0].at[peer] if axis < order[0] else held[0].at[:, peer]
                else:
                    source = held[1].at[peer]
                remote(source, landing[stage].at[k - 1], slot + 3 * p + stage, along_axis(axis, peer))
            pending.append((landing[stage], stage_send.at[slot + 3 * p + stage]))

    def scatter_sum(slot, buffer, rooms, cuts, stage, finish=None):
        for p, order in enumerate(GATHER_ORDERS):
            axis = order[2 - stage]
            landing, held = rooms[p]
            wait_bytes(landing[stage], stage_recv.at[slot + 3 * p + stage])
            if stage == 0:
                where = [slice(None)] * 3
                where[axis] = me[axis]
                mine = buffer[(*where, *cuts[p])]
            elif stage == 1:
                mine = held[0][me[axis]] if axis < order[0] else held[0][:, me[axis]]
            else:
                mine = held[1][me[axis]]
            value = mine.astype(F32)
            for k in range(GRID[axis] - 1):
                value = value + landing[stage][k].astype(F32)
            if stage == 2:
                finish(cuts[p], value)
            else:
                held[stage][...] = value.astype(BF16)

    def over_grp(slot, source, target):
        def step(k, carry):
            peer = lax.rem(me_g + k, n_grp)
            pltpu.make_async_remote_copy(
                src_ref=source(peer),
                dst_ref=target(k),
                send_sem=send_sem.at[slot],
                recv_sem=recv_sem.at[slot],
                device_id={"grp": peer},
                device_id_type=MESH,
            ).start()
            return carry

        lax.fori_loop(1, n_grp, step, 0)

    mate = me_t + 1 - 2 * (me_t % 2)
    across = lax.rem(me_t + n_tp // 2, n_tp)

    def to_tp(slot, source, target, peer):
        pltpu.make_async_remote_copy(
            src_ref=source,
            dst_ref=target,
            send_sem=tp_send.at[slot],
            recv_sem=tp_recv.at[slot],
            device_id={"tp": peer},
            device_id_type=MESH,
        ).start()
        pending.append((source, tp_send.at[slot]))

    def tp_first(slot, source, buffer):
        to_tp(slot, source, buffer.at[me_t], across)
        to_tp(slot + 1, source, buffer.at[me_t], mate)

    def tp_second(slot, buffer):
        wait_bytes(buffer.at[across], tp_recv.at[slot])
        to_tp(slot + 2, buffer.at[across], buffer.at[across], mate)

    def tp_last(slot, buffer):
        wait_bytes(buffer.at[0], tp_recv.at[slot + 1])
        wait_bytes(buffer.at[0], tp_recv.at[slot + 2])

    def arrived(slot, buffer):
        part = buffer.at[pl.ds(0, buffer.shape[0] - 1)]
        pltpu.make_async_copy(part, part, recv_sem.at[slot]).wait()

    def sent(slot, buffer):
        part = buffer.at[pl.ds(0, buffer.shape[0] - 1)]
        pltpu.make_async_copy(part, part, send_sem.at[slot]).wait()

    def summed_slots(first, recv):
        def add(k, total):
            return total + recv[k].astype(F32)

        return lax.fori_loop(1, n_grp, add, first.astype(F32))

    barrier = pltpu.get_barrier_semaphore()

    def greet(k, carry):
        pl.semaphore_signal(
            barrier, inc=1, device_id={"grp": lax.rem(me_g + k, n_grp)}, device_id_type=MESH
        )
        return carry

    lax.fori_loop(1, n_grp, greet, 0)
    for k in range(1, n_tp):
        pl.semaphore_signal(
            barrier, inc=1, device_id={"tp": lax.rem(me_t + k, n_tp)}, device_id_type=MESH
        )
    load_state = pltpu.make_async_copy(state_hbm, state_v, load_sem.at[0])
    load_inject = pltpu.make_async_copy(inject_hbm, inject_v, load_sem.at[1])
    load_down = pltpu.make_async_copy(down_hbm, down_v, load_sem.at[2])
    tall_load = pltpu.make_async_copy(tall_ref, tall_v.at[me], load_sem.at[3])
    tall_load.start()
    load_state.start()
    load_inject.start()
    load_down.start()

    def up_copy(i):
        rows = pl.ds(pl.multiple_of(i * ROWS, ROWS), ROWS)
        return pltpu.make_async_copy(up_hbm.at[rows], up_v.at[rows], up_sem.at[i])

    chunks = hidden // ROWS
    pl.semaphore_wait(barrier, n_grp - 1 + n_tp - 1)

    tp_first(0, pair_ref, pairs_v)
    pairs_v[me_t] = pair_ref[...]
    tall_load.wait()
    gather_start(0, tall_v, F_CUTS, 0)
    m_rooms, g_rooms, f_rooms = stages

    load_state.wait()
    load_inject.wait()
    for i in range(chunks):
        up_copy(i).start()
    step_rows = 160

    def add_rows(i, square):
        rows = pl.ds(pl.multiple_of(i * step_rows, step_rows), step_rows)
        value = state_v[rows].astype(F32) + inject_v[rows].astype(F32)
        summed_v[rows] = value
        return square + (value * value).reshape(step_rows // 8, 8, tokens).sum(axis=0)

    square = lax.fori_loop(0, width // step_rows, add_rows, jnp.zeros((8, tokens), F32))
    summed_v[pl.ds(width, 16)] = jnp.zeros((16, tokens), F32)
    square = square.sum(axis=0, keepdims=True)
    mean1 = square / width + epsilon
    rho1 = lax.rsqrt(mean1)
    norm1 = jnp.sqrt(mean1)

    tp_second(0, pairs_v)
    gather_wait(0, tall_v, F_CUTS, 0)
    gather_start(0, tall_v, F_CUTS, 1)

    def scale_rows(i, carry):
        rows = pl.ds(pl.multiple_of(i * step_rows, step_rows), step_rows)
        normed_v[rows] = (summed_v[rows] * rho1).astype(BF16)
        return carry

    lax.fori_loop(0, width // step_rows, scale_rows, 0)

    tp_last(0, pairs_v)
    up_cols = pairs_v[:, :own].reshape(units, cols)
    down_cols = pairs_v[:, own:].reshape(units, cols)
    own_down = pair_ref[own:]
    grams = jnp.concatenate([dot(own_down, down_cols, NT), dot(own_down, up_cols, NT)], axis=0)
    half = n_grp // 2
    k_send[:half] = grams[:, :TILE].reshape(half, 8, TILE)
    k_send[half:] = grams[:, TILE:].reshape(half, 8, TILE)
    over_grp(1, lambda p: k_send.at[p], lambda k: k_recv.at[k])
    load_down.wait()
    spans = [(c, min(640, hidden - c)) for c in range(0, hidden, 640)]
    for c, w in spans:
        part = dot(down_cols, down_v[:, c : c + w])
        m_send[:, :, :, :, c : c + w] = part.reshape(*GRID, 8, w).astype(BF16)
    blank = jnp.zeros((*GRID, 8, wide - hidden), BF16)
    m_send[:, :, :, :, hidden:wide] = blank
    gather_wait(0, tall_v, F_CUTS, 1)
    gather_start(0, tall_v, F_CUTS, 2)
    scatter_start(9, m_send, m_rooms, M_CUTS, 0)

    def block_rows(i, carry):
        for part in range(8):
            base = pl.multiple_of(i * (8 * cols) + part * cols // 8 * 8, 8)
            value = summed_v[pl.ds(base, tall + 8)]
            shift = part * cols % 8
            blocks_v[i * 8 + part] = (value[shift : shift + tall] * rho1).astype(BF16)
        return carry

    lax.fori_loop(0, n_grp // 8, block_rows, 0)

    def up_rows(i, carry):
        up_copy(i).wait()
        rows = pl.ds(pl.multiple_of(i * ROWS, ROWS), ROWS)
        hidden_v[rows] = jax.nn.silu(dot(up_v[rows], normed_v[...])).astype(BF16)
        return carry

    lax.fori_loop(0, 2, up_rows, 0)
    arrived(1, k_recv)
    k_full[me_g] = summed_slots(k_send[me_g], k_recv)
    over_grp(2, lambda p: k_full.at[me_g], lambda k: k_full.at[me_g])
    scatter_sum(9, m_send, m_rooms, M_CUTS, 0)
    scatter_start(9, m_send, m_rooms, M_CUTS, 1)
    lax.fori_loop(2, 5, up_rows, 0)
    scatter_sum(9, m_send, m_rooms, M_CUTS, 1)
    scatter_start(9, m_send, m_rooms, M_CUTS, 2)
    lax.fori_loop(5, chunks, up_rows, 0)

    def into(buffer):
        def finish(cut, value):
            buffer[(*me, *cut)] = value.astype(BF16)

        return finish

    gather_wait(0, tall_v, F_CUTS, 2)
    group = GRID[1] * GRID[2]

    def logit_rows(j, total):
        a = tall_v[j].reshape(group * tall, 2 * own)
        b = blocks_v[pl.ds(j * group, group)].reshape(group * tall, tokens)
        return total + dot(a, b, TN)

    z_all[me_t] = lax.fori_loop(0, GRID[0], logit_rows, jnp.zeros((2 * own, tokens), F32))
    tp_first(3, z_all.at[me_t], z_all)
    scatter_sum(9, m_send, m_rooms, M_CUTS, 2, into(m_full))
    gather_start(18, m_full, M_CUTS, 0)
    arrived(2, k_full)
    low = k_full[:half].reshape(2 * own, TILE)
    high = k_full[half:].reshape(2 * own, TILE)
    small_all[me_t] = jnp.concatenate([low, high], axis=1)
    tp_first(6, small_all.at[me_t], small_all)
    tp_second(3, z_all)
    tp_second(6, small_all)
    gather_wait(18, m_full, M_CUTS, 0)
    gather_start(18, m_full, M_CUTS, 1)

    tp_last(3, z_all)
    tp_last(6, small_all)
    gram_f = small_all[:, :own].reshape(units, units)
    gram_hi = gram_f.astype(BF16)
    gram_lo = (gram_f - gram_hi.astype(F32)).astype(BF16)
    cross = small_all[:, own:].reshape(units, units).astype(BF16)

    def gram_dot(value):
        return dot(gram_hi, value) + dot(gram_lo, value)

    logits1 = z_all[:, :own].reshape(units, tokens)
    along = z_all[:, own:].reshape(units, tokens) * norm1
    upward = logits1 * norm1
    sequence = me_g * tokens // LENGTH
    taught = jnp.where(step_ref[sequence] == 1, 1.0, 0.0)
    deep = jnp.where(depth_ref[sequence] == 2, 1.0, 0.0)
    hidden1 = jax.nn.silu(logits1).astype(BF16)
    gram1 = gram_dot(hidden1)
    hidden1_f = hidden1.astype(F32)
    moved = along + gram1
    square2 = square + jnp.sum(hidden1_f * (along + moved), axis=0, keepdims=True)
    rho2 = lax.rsqrt(jnp.maximum(square2, 0.0) / width + epsilon)
    upward2 = upward + dot(cross, hidden1, TN)
    logits2 = upward2 * rho2
    hidden2 = (jax.nn.silu(logits2) * deep).astype(BF16)
    total_f = hidden1_f + hidden2.astype(F32)
    total = total_f.astype(BF16)
    taught_total = (total_f * taught).astype(BF16)
    for c, w in spans:
        part = dot(taught_total, hidden_v[c : c + w], NT) * (-scale)
        g_send[:, :, :, :, c : c + w] = part.reshape(*GRID, 8, w).astype(BF16)
    g_send[:, :, :, :, hidden:wide] = blank
    scatter_start(27, g_send, g_rooms, M_CUTS, 0)

    gather_wait(18, m_full, M_CUTS, 1)
    gather_start(18, m_full, M_CUTS, 2)
    scatter_sum(27, g_send, g_rooms, M_CUTS, 0)
    scatter_start(27, g_send, g_rooms, M_CUTS, 1)
    gather_wait(18, m_full, M_CUTS, 2)

    teach = m_full[:, :, :, :, :hidden].reshape(units, hidden)
    term = dot(teach, hidden_v[...])
    term_send[...] = term.astype(BF16)
    to_tp(9, term_send, term_recv, mate)
    core = me_t % 2
    core_rows = pl.ds(pl.multiple_of(core * TILE, TILE), TILE)
    wait_bytes(term_recv, tp_recv.at[9])
    term_f32[...] = term + term_recv[...].astype(F32)
    half_send[...] = term_f32[core_rows].astype(BF16)
    to_tp(10, half_send, half_recv, across)
    scatter_sum(27, g_send, g_rooms, M_CUTS, 1)
    scatter_start(27, g_send, g_rooms, M_CUTS, 2)
    wait_bytes(half_recv, tp_recv.at[10])
    term_sum[core] = term_f32[core_rows] + half_recv[...].astype(F32)
    to_tp(11, term_sum.at[core], term_sum.at[core], mate)
    scatter_sum(27, g_send, g_rooms, M_CUTS, 2, into(g_full))
    gather_start(45, g_full, M_CUTS, 0)
    wait_bytes(term_sum.at[0], tp_recv.at[11])
    term = term_sum[...].reshape(units, tokens)

    slope = scale * (gram1 + gram_dot(hidden2) - term * taught)
    q2 = slope * silu_slope(logits2) * deep
    mu = jnp.sum(upward2 * q2, axis=0, keepdims=True) / width
    rq2 = (rho2 * q2).astype(BF16)
    ratio = rho2 * rho2 * rho2 * mu
    slope1 = slope + dot(cross, rq2) - ratio * moved
    q1 = slope1 * silu_slope(logits1)
    rq2_f = rq2.astype(F32)
    keep[0] = q1 + rq2_f * norm1
    keep[1] = -hidden1_f * (ratio * norm1)
    keep[2] = total_f
    keep[3] = hidden1_f * ratio
    keep[4] = hidden1_f
    keep[5] = rq2_f
    mine = pl.ds(pl.multiple_of(me_t * own, own), own)
    left = jnp.concatenate([keep[0, mine], keep[1, mine]], axis=0).astype(BF16)

    def direct_rows(j, carry):
        b = blocks_v[pl.ds(j * group, group)].reshape(group * tall, tokens)
        f_send[j] = dot(b, left, NT).reshape(*GRID[1:], tall, 2 * own).astype(BF16)
        return carry

    lax.fori_loop(0, GRID[0], direct_rows, 0)
    c1 = scale * dot(keep[2, mine].astype(BF16), total, NT) - dot(keep[3, mine].astype(BF16), hidden1, NT)
    c2 = dot(keep[4, mine].astype(BF16), rq2, NT)
    c3 = dot(keep[5, mine].astype(BF16), hidden1, NT)
    folded = jnp.concatenate([c1, c2, c3, jnp.zeros((own, units), F32)], axis=0)
    c_send[...] = folded.reshape(n_grp, 8, units).astype(BF16)
    over_grp(8, lambda p: c_send.at[p], lambda k: c_recv.at[k])
    scatter_start(36, f_send, f_rooms, F_CUTS, 0)
    gather_wait(45, g_full, M_CUTS, 0)
    gather_start(45, g_full, M_CUTS, 1)
    arrived(8, c_recv)
    c_full[me_g] = summed_slots(c_send[me_g], c_recv).astype(BF16)
    over_grp(11, lambda p: c_full.at[me_g], lambda k: c_full.at[me_g])
    gather_wait(45, g_full, M_CUTS, 1)
    gather_start(45, g_full, M_CUTS, 2)
    scatter_sum(36, f_send, f_rooms, F_CUTS, 0)
    scatter_start(36, f_send, f_rooms, F_CUTS, 1)

    def to_direct(cut, value):
        direct_ref[cut] = value

    scatter_sum(36, f_send, f_rooms, F_CUTS, 1)
    scatter_start(36, f_send, f_rooms, F_CUTS, 2)
    gather_wait(45, g_full, M_CUTS, 2)
    outer = g_full[:, :, :, :, :hidden].reshape(units, hidden)
    out_part[...] = dot(outer, down_v[...], NT).reshape(2, 2, own, cols)
    to_tp(12, out_part.at[:, 1 - core], out_pair, mate)
    scatter_sum(36, f_send, f_rooms, F_CUTS, 2, to_direct)
    wait_bytes(out_pair, tp_recv.at[12])
    out_send[...] = out_part[across // 2, core] + out_pair[across // 2]
    to_tp(13, out_send, out_last, across)
    arrived(11, c_full)
    folded = c_full[...].reshape(units, units)
    up_cols = pairs_v[:, :own].reshape(units, cols)
    down_cols = pairs_v[:, own:].reshape(units, cols)
    down_rest = dot(folded[:own], down_cols) + dot(folded[own : 2 * own], up_cols)
    rest_ref[:own] = dot(folded[2 * own : 3 * own], down_cols)
    down_rest = down_rest + out_part[me_t // 2, core] + out_pair[me_t // 2]
    wait_bytes(out_last, tp_recv.at[13])
    rest_ref[own:] = down_rest + out_last[...]

    sent(1, k_recv)
    sent(2, k_full)
    sent(8, c_recv)
    sent(11, c_full)
    for part, sem in pending:
        wait_bytes(part, sem)


def body(
    teacher_state,
    injection,
    teacher_up,
    teacher_down,
    student_up,
    student_down,
    teacher_step,
    student_depth,
):
    n_tp, n_grp = lax.axis_size("tp"), lax.axis_size("grp")
    tokens, width = teacher_state.shape
    cols, own = student_up.shape
    units = own * n_tp
    hidden = teacher_down.shape[0]
    scale = loss_scale * 2.0 / (tokens * n_grp)
    tall = ceil_to(cols, 16)
    wide = ceil_to(hidden, TILE)

    pair = jnp.concatenate([student_up.T, student_down], axis=0)
    tall_pair = jnp.pad(pair.T, ((0, tall - cols), (0, 0)))
    any_spec = pl.BlockSpec(memory_space=pl.ANY)
    vmem = pl.BlockSpec(memory_space=pltpu.VMEM)
    smem = pl.BlockSpec(memory_space=pltpu.SMEM)
    chunk = (*GRID, 8, wide)
    direct, rest = pl.pallas_call(
        functools.partial(kernel, n_tp, n_grp, (tokens, width, cols, own, hidden, wide, scale)),
        out_shape=(
            jax.ShapeDtypeStruct((tall, 2 * own), F32),
            jax.ShapeDtypeStruct((2 * own, cols), F32),
        ),
        in_specs=[any_spec] * 4 + [vmem] * 2 + [smem] * 2,
        out_specs=(vmem, vmem),
        scratch_shapes=[
            pltpu.VMEM((width, tokens), BF16),
            pltpu.VMEM((width, tokens), BF16),
            pltpu.VMEM((hidden, width), BF16),
            pltpu.VMEM((cols, hidden), BF16),
            pltpu.VMEM((width + 16, tokens), F32),
            pltpu.VMEM((width, tokens), BF16),
            pltpu.VMEM((n_grp, tall, tokens), BF16),
            pltpu.VMEM((hidden, tokens), BF16),
            pltpu.VMEM((n_tp, 2 * own, cols), BF16),
            pltpu.VMEM((*GRID, tall, 2 * own), BF16),
            pltpu.VMEM(chunk, BF16),
            pltpu.VMEM(chunk, BF16),
            pltpu.VMEM(chunk, BF16),
            pltpu.VMEM(chunk, BF16),
            pltpu.VMEM((n_grp, 8, units), BF16),
            pltpu.VMEM((n_grp, 8, units), BF16),
            pltpu.VMEM((n_grp, 8, units), BF16),
            pltpu.VMEM((n_grp, 8, TILE), F32),
            pltpu.VMEM((n_grp, 8, TILE), F32),
            pltpu.VMEM((n_grp, 8, TILE), F32),
            pltpu.VMEM((*GRID, tall, 2 * own), BF16),
            (
                room_shapes(8, wide, M_CUTS),
                room_shapes(8, wide, M_CUTS),
                room_shapes(tall, 2 * own, F_CUTS),
            ),
            pltpu.VMEM((n_tp, 2 * own, tokens), F32),
            pltpu.VMEM((n_tp, 2 * own, units), F32),
            pltpu.VMEM((units, tokens), F32),
            pltpu.VMEM((units, tokens), BF16),
            pltpu.VMEM((units, tokens), BF16),
            pltpu.VMEM((units // 2, tokens), BF16),
            pltpu.VMEM((units // 2, tokens), BF16),
            pltpu.VMEM((2, units // 2, tokens), F32),
            pltpu.VMEM((2, 2, own, cols), F32),
            pltpu.VMEM((2, own, cols), F32),
            pltpu.VMEM((own, cols), F32),
            pltpu.VMEM((own, cols), F32),
            pltpu.VMEM((6, units, tokens), F32),
            pltpu.SemaphoreType.DMA((4,)),
            pltpu.SemaphoreType.DMA((hidden // ROWS,)),
            pltpu.SemaphoreType.DMA((13,)),
            pltpu.SemaphoreType.DMA((13,)),
            pltpu.SemaphoreType.DMA((54,)),
            pltpu.SemaphoreType.DMA((54,)),
            pltpu.SemaphoreType.DMA((14,)),
            pltpu.SemaphoreType.DMA((14,)),
        ],
        compiler_params=pltpu.CompilerParams(
            collective_id=0, has_side_effects=True, vmem_limit_bytes=67043328
        ),
    )(teacher_state.T, injection.T, teacher_up.T, teacher_down.T, tall_pair, pair, teacher_step, student_depth)
    grad_up = direct[:cols, :own] + rest[:own].T
    grad_down = direct[:cols, own:].T + rest[own:]
    return (grad_up, grad_down)


def solution(mesh):
    in_specs = (
        P("grp", None),
        P("grp", None),
        P(None, "tp"),
        P("tp", "grp"),
        P("grp", "tp"),
        P("tp", "grp"),
        P(),
        P(),
    )
    out_specs = (P("grp", "tp"), P("tp", "grp"))
    return jax.shard_map(body, mesh=mesh, in_specs=in_specs, out_specs=out_specs, check_vma=False)
```

time: 150 us -> 106 us (0.71)
  the two profiles are of different devices: /device:TPU:5 before, /device:TPU:1 now
where the time goes in v3:
time: 106 us; the launch traced here: 104 us
  Pallas kernels  97.7 us (92%)
  other arithmetic  4.37 us (4%)
  local copies, waits for them, and re-layouts  1.73 us (2%)
    pallas_call x1, Pallas kernels, body(): pl.pallas_call(functools.partial(kernel, n_tp, n_grp, (tokens, width, col...  97.7 us

profile of v3, /device:TPU:1, one launch (start us, length us, event | category | flops | bytes accessed | tf_op | source)
XLA Modules:
  0.0 104.5 jit_solution(16549423046243781751)
XLA Ops:
  0.6 1.4 %pad_maximum_fusion = (bf16[128,165]{1,0:T(8,128)(2,1)}, bf16[165,128]{0,1:T(8,128)(2,1)S(1)}) fusion(bf16[64,165]{1,0:T(8,128)(2,1)} %param.13, bf16[64,165]{1,0:T(8,128)(2,1)} %bitcast.17), kind=kLoop, calls=%fused_computation.3 | loop fusion | flops 84480 | bytes 126720 | tf_op jit(solution)/shard_map/concatenate | solution.py:557
  2.0 0.1 copy.13
  2.2 0.6 pad.4.clone.tall_ref
  2.8 97.7 %shard_map.95 = (f32[176,128]{1,0:T(8,128)}, f32[128,165]{1,0:T(8,128)}) custom-call(bf16[5280,256]{1,0:T(8,128)(2,1)} %bitcast.14, bf16[5280,256]{1,0:T(8,128)(2,1)} %bitcast.15, bf16[2240,5280]{1,0:T(8,128)(2,1)} %bitcast.13, bf16[165,2240]{1,0:T(8,128)(2,1)} %bitcast.16, bf16[176,128]{1,0:T(8,128)(2,1)} %pad.4.clone.tall_ref, ...), custom_call_target="tpu_custom_call" | custom-call | tf_op jit(solution)/shard_map/pallas_call | solution.py:563
  100.5 1.0 copy.11
  101.5 1.5 %fusion = f32[64,165]{1,0:T(8,128)} fusion(f32[176,128]{0,1:T(8,128)S(1)} %copy.11, f32[128,165]{1,0:T(8,128)} %get-tuple-element.5), kind=kLoop, calls=%fused_computation.1 | loop fusion | flops 10560 | bytes 126720 | tf_op jit(solution)/shard_map/add | solution.py:625
  103.0 1.5 %slice_add_fusion = f32[165,64]{0,1:T(8,128)} fusion(f32[176,128]{0,1:T(8,128)S(1)} %copy.11, f32[128,165]{1,0:T(8,128)} %get-tuple-element.5), kind=kLoop, calls=%fused_computation.2 | loop fusion | flops 10560 | bytes 126720 | tf_op jit(solution)/shard_map/add | solution.py:624
